TPU v7x, 128 devices: a whole 4x4x4 slice. The times are simulated.
128 devices in a mesh: gx: 8 (over y, core), yz: 16 (over x, z).
Axes of the slice: x: 4, y: 4, z: 4, core: 2. Of those that a mesh axis runs over, the one named last changes fastest.
Arguments:
- gas_state: float32 [5, 128, 256, 256], P(None, 'gx', 'yz'), may hold values from -6 to 6
- parcel_speed: float32 [8, 16, 128, 4, 3, 128], P('gx', 'yz'), may hold values from -6 to 6
- parcel_mass: float32 [8, 16, 128, 4, 128], P('gx', 'yz'), may hold values from 0.3 to 3
- offsets: float32 [8, 16, 128, 4, 3, 128], P('gx', 'yz'), may hold values from 0 to 1
- cell_base: int32 [8, 16, 128, 4, 3, 128], P('gx', 'yz'), may hold values from 0 to 6, as said below
- block_tile: int32 [8, 16, 128, 4], P('gx', 'yz'), may hold values from 0 to 511
- block_count: int32 [8, 16, 128], P('gx', 'yz'), may hold values from 0 to 4, as said below
Outputs:
- gas_next: float32 [5, 128, 256, 256], P(None, 'gx', 'yz')
- speed_next: float32 [8, 16, 128, 4, 3, 128], P('gx', 'yz')
- mass_next: float32 [8, 16, 128, 4, 128], P('gx', 'yz')
Inputs may be any that keep to these rules, and one draw needn't show every extreme that they name: `block_count`: A device's live blocks for an owner are its first ones; in every draw some owner receives 4 live blocks from every device. `cell_base`: component 0, 1, 2 is at most 2, 2, 6, so that the base cell and the next cell along each dimension lie in the tile.
All inputs are finite; a program needn't handle non-finite values.
Results may differ from a plain program's by a relative error of at most 0.0003.
Values sent between devices are 32-bit elements; how exact they have to be, the bound alone decides.
A program may use at most 128 MiB of HBM per device.

v0:
```python
import math

import jax
import jax.numpy as jnp
from jax import lax
from jax.sharding import PartitionSpec as P

TILE_X = 4
TILE_Y = 4
TILE_Z = 8


DIFFUSION = 0.1
CELL_MASS = 4.0
DRAG_RATE = 0.5
EVAPORATION = 0.3
LATENT_HEAT = 2.0


def with_halo(value, sides, width):
    edges = {}
    for axis, dim in sides:
        count, length = (lax.axis_size(axis), value.shape[dim])
        up = [(i, (i + 1) % count) for i in range(count - 1)]
        last = lax.slice_in_dim(value, length - width, length, axis=dim)
        initial = lax.slice_in_dim(value, 0, width, axis=dim)
        edges[dim] = (
            lax.ppermute(last, axis, up),
            lax.ppermute(initial, axis, [(b, a) for a, b in up]),
        )
    done = []
    for _, dim in sides:
        low, high = edges[dim]
        around = [(width, width) if d in done else (0, 0) for d in range(value.ndim)]
        value = jnp.concatenate([jnp.pad(low, around), value, jnp.pad(high, around)], axis=dim)
        done.append(dim)
    return value


def split_tiles(block):
    fields, extent_x, extent_y, extent_z = block.shape
    grid = block.reshape(
        fields, extent_x // TILE_X, TILE_X, extent_y // TILE_Y, TILE_Y, extent_z // TILE_Z, TILE_Z
    )
    grid = grid.transpose(1, 3, 5, 0, 2, 4, 6)
    return grid.reshape(-1, fields, TILE_X * TILE_Y * TILE_Z)


def join_tiles(tile_data, extent_x, extent_y, extent_z):
    fields = tile_data.shape[1]
    grid = tile_data.reshape(
        extent_x // TILE_X, extent_y // TILE_Y, extent_z // TILE_Z, fields, TILE_X, TILE_Y, TILE_Z
    )
    return grid.transpose(3, 0, 4, 1, 5, 2, 6).reshape(fields, extent_x, extent_y, extent_z)


def laplace(padded):
    framed = jnp.pad(padded, ((0, 0), (0, 0), (0, 0), (1, 1)))
    centre = framed[:, 1:-1, 1:-1, 1:-1]
    beside_all = framed[:, 2:, 1:-1, 1:-1] + framed[:, :-2, 1:-1, 1:-1]
    beside_all = beside_all + framed[:, 1:-1, 2:, 1:-1] + framed[:, 1:-1, :-2, 1:-1]
    beside_all = beside_all + framed[:, 1:-1, 1:-1, 2:] + framed[:, 1:-1, 1:-1, :-2]
    return beside_all - 6.0 * centre


def weights_along(fraction, base_cell, extent):
    positions = jnp.arange(extent, dtype=jnp.int32)
    lower_hit = (base_cell[..., None] == positions).astype(jnp.float32)
    upper_hit = (base_cell[..., None] + 1 == positions).astype(jnp.float32)
    return (1.0 - fraction)[..., None] * lower_hit + fraction[..., None] * upper_hit


def parcel_update(tile_data, velocity, shifts, cells, mass_old, live):
    along_x = weights_along(shifts[:, 0], cells[:, 0], TILE_X)
    along_y = weights_along(shifts[:, 1], cells[:, 1], TILE_Y)
    along_z = weights_along(shifts[:, 2], cells[:, 2], TILE_Z)
    stencil = (
        along_x[:, :, :, None, None] * along_y[:, :, None, :, None] * along_z[:, :, None, None, :]
    )
    stencil = stencil.reshape(mass_old.shape + (TILE_X * TILE_Y * TILE_Z,))
    sampled = jnp.einsum("scq,spq->scp", tile_data, stencil, precision=lax.Precision.HIGHEST)
    radius = jnp.cbrt(mass_old)
    factor = DRAG_RATE / (radius * radius)
    alive = live > 0.5
    moved = (velocity + factor[:, None, :] * sampled[:, 0:3]) / (1.0 + factor[:, None, :])
    velocity_new = jnp.where(alive[:, None, None], moved, velocity)
    evap_loss = EVAPORATION * jax.nn.softplus(sampled[:, 3] - sampled[:, 4]) / radius
    mass_new = jnp.where(alive[:, None], mass_old / (1.0 + evap_loss), mass_old)
    vapour = mass_old - mass_new
    momentum = mass_old[:, None, :] * (velocity - velocity_new) + vapour[:, None, :] * velocity_new
    source = jnp.concatenate(
        [momentum, -LATENT_HEAT * vapour[:, None, :], vapour[:, None, :]], axis=1
    )
    source = source * live[:, None, None]
    deposit = jnp.einsum("scp,spq->scq", source, stencil, precision=lax.Precision.HIGHEST)
    return (velocity_new, mass_new, deposit)


def in_groups(tile_data, velocity, shifts, cells, mass_old, live):
    leading = live.shape
    slot_total = leading[0] * leading[1]
    group_size = math.gcd(slot_total, 64)

    def grouped(member):
        return member.reshape((slot_total // group_size, group_size) + member.shape[2:])

    def process(packed):
        return parcel_update(*packed)

    outcome = lax.map(
        process,
        tuple((grouped(member) for member in (tile_data, velocity, shifts, cells, mass_old, live))),
    )
    return tuple((member.reshape(leading + member.shape[2:]) for member in outcome))


def shards(gas_state, parcel_speed, parcel_mass, offsets, cell_base, block_tile, block_count):
    fields, extent_x, extent_y, extent_z = gas_state.shape
    devices, capacity = (block_tile.shape[2], block_tile.shape[3])
    slot_total = devices * capacity
    table = split_tiles(gas_state)
    tile_rows = table.shape[0]
    padded = with_halo(gas_state, (("gx", 1), ("yz", 2)), 1)
    diffused = laplace(padded)
    velocity = parcel_speed.reshape(devices, capacity, 3, -1)
    mass_old = parcel_mass.reshape(devices, capacity, -1)
    shifts = offsets.reshape(devices, capacity, 3, -1)
    cells = cell_base.reshape(devices, capacity, 3, -1)
    tile_index = block_tile.reshape(devices, capacity)
    counted = block_count.reshape(devices)
    live = lax.broadcasted_iota(jnp.int32, (devices, capacity), 1) < counted[:, None]
    wanted = lax.all_to_all(tile_index, ("gx", "yz"), split_axis=0, concat_axis=0, tiled=True)
    fetched = lax.all_to_all(table[wanted], ("gx", "yz"), split_axis=0, concat_axis=0, tiled=True)
    velocity_new, mass_new, deposit = in_groups(
        fetched, velocity, shifts, cells, mass_old, live.astype(jnp.float32)
    )
    arrived = lax.all_to_all(deposit, ("gx", "yz"), split_axis=0, concat_axis=0, tiled=True)
    summed = jax.ops.segment_sum(
        arrived.reshape(slot_total, fields, -1), wanted.reshape(-1), num_segments=tile_rows
    )
    source_field = join_tiles(summed, extent_x, extent_y, extent_z)
    gas_next = gas_state + DIFFUSION * diffused + source_field / CELL_MASS
    return (gas_next, velocity_new.reshape(parcel_speed.shape), mass_new.reshape(parcel_mass.shape))


def solution(mesh):
    in_specs = (
        P(None, "gx", "yz", None),
        P("gx", "yz", None, None, None, None),
        P("gx", "yz", None, None, None),
        P("gx", "yz", None, None, None, None),
        P("gx", "yz", None, None, None, None),
        P("gx", "yz", None, None),
        P("gx", "yz", None),
    )
    out_specs = (
        P(None, "gx", "yz", None),
        P("gx", "yz", None, None, None, None),
        P("gx", "yz", None, None, None),
    )
    return jax.shard_map(shards, mesh=mesh, in_specs=in_specs, out_specs=out_specs, check_vma=False)
```

profile of v0, /device:TPU:1, one launch (start us, length us, event | category | flops | bytes accessed | tf_op | source)
XLA Modules:
  0.0 335.0 jit_solution(7024749568511878126)
XLA Ops:
  2.0 11.5 %all-to-all-start = ((s32[128,1,4]{2,1,0:T(1,128)}), s32[128,1,4]{2,1,0:T(1,128)S(1)}, u32[]{:S(2)}, u32[]{:S(2)}) async-start(s32[128,1,4]{2,1,0:T(1,128)} %bitcast.18), calls=%async_computation | async-start | bytes 131072 | tf_op jit(solution)/shard_map/all_to_all | solution.py:132
  13.5 14.5 %reshape.245 = f32[5,4,4,4,4,32,8]{6,5,4,3,2,1,0:T(8,128)} reshape(f32[5,16,16,256]{3,2,1,0:T(8,128)} %param.9) | data formatting | bytes 2621440 | tf_op jit(solution)/shard_map/reshape | solution.py:42
  28.0 14.1 %copy.98 = f32[4,4,32,5,4,4,8]{2,1,0,6,5,4,3:T(4,128)} copy(f32[4,4,32,5,4,4,8]{6,2,5,1,4,0,3:T(8,128)} %bitcast.148) | data formatting | bytes 2621440 | tf_op jit(solution)/shard_map/transpose | solution.py:45
  42.1 6.5 %reshape.246 = f32[512,5,128]{0,2,1:T(8,128)S(1)} reshape(f32[4,4,32,5,4,4,8]{2,1,0,6,5,4,3:T(4,128)} %copy.98) | data formatting | bytes 2621440 | tf_op jit(solution)/shard_map/reshape | solution.py:46
  55.4 9.8 %all-to-all-start.1 = ((f32[128,4,5,128]{3,1,2,0:T(4,128)}), f32[128,4,5,128]{3,1,2,0:T(4,128)S(1)}, u32[]{:S(2)}, u32[]{:S(2)}) async-start(f32[128,4,5,128]{3,1,2,0:T(4,128)} %copy.101), calls=%async_computation.1 | async-start | bytes 2621440 | tf_op jit(solution)/shard_map/all_to_all | solution.py:133
  69.3 17.2 %all-to-all-done.1 = f32[128,4,5,128]{3,1,2,0:T(4,128)S(1)} async-done(((f32[128,4,5,128]{3,1,2,0:T(4,128)}), f32[128,4,5,128]{3,1,2,0:T(4,128)S(1)}, u32[]{:S(2)}, u32[]{:S(2)}) %all-to-all-start.1) | async-done | bytes 1310752 | tf_op jit(solution)/shard_map/all_to_all | solution.py:133
  87.7 135.7 %while.14 = (s32[]{:T(128)}, f32[8,64,3,128]{3,2,1,0:T(4,128)}, f32[8,64,128]{2,1,0:T(8,128)}, f32[8,64,5,128]{3,2,1,0:T(8,128)}, f32[8,64]{1,0:T(8,128)S(1)}, /...) while((s32[]{:T(128)}, f32[8,64,3,128]{3,2,1,0:T(4,128)}, ...), condition=%wide.region_1.2_spmd, body=%wide.region_0.1_spmd.sunk | while | flops 128376896 | bytes 18614980 | solution.py:110
  95.8 7.4 %fusion.48 = f32[8,64,5,128]{3,2,1,0:T(8,128)} fusion(f32[8,64,5,128]{3,2,1,0:T(8,128)} %get-tuple-element.287, s32[]{:T(128)} %get-tuple-element.284, f32[64,128,128]{1,2,0:T(8,128)S(1)} %bitcast.147, f32[64,1,128]{2,1,0:T(1,128)S(1)} %get-tuple-element.270, f32[64,1,128]{2,1,0:T(1,128)S(1)} %get-tuple-element.271, f32[64,3,128]{2,1,0:T(4,128)S(1)} %fusion.47, ...), kind=kOutput, calls=%fused_computation.4.clone.1 | convolution fusion | flops 63037440 | bytes 4621056 | tf_op jit(solution)/shard_map/while/body/eval_jaxpr/scp,spq->scq/dot_general | solution.py:95
  112.8 7.4 %fusion.48 = f32[8,64,5,128]{3,2,1,0:T(8,128)} fusion(f32[8,64,5,128]{3,2,1,0:T(8,128)} %get-tuple-element.287, s32[]{:T(128)} %get-tuple-element.284, f32[64,128,128]{1,2,0:T(8,128)S(1)} %bitcast.147, f32[64,1,128]{2,1,0:T(1,128)S(1)} %get-tuple-element.270, f32[64,1,128]{2,1,0:T(1,128)S(1)} %get-tuple-element.271, f32[64,3,128]{2,1,0:T(4,128)S(1)} %fusion.47, ...), kind=kOutput, calls=%fused_computation.4.clone.1 | convolution fusion | flops 63037440 | bytes 4621056 | tf_op jit(solution)/shard_map/while/body/eval_jaxpr/scp,spq->scq/dot_general | solution.py:95
  129.8 7.4 %fusion.48 = f32[8,64,5,128]{3,2,1,0:T(8,128)} fusion(f32[8,64,5,128]{3,2,1,0:T(8,128)} %get-tuple-element.287, s32[]{:T(128)} %get-tuple-element.284, f32[64,128,128]{1,2,0:T(8,128)S(1)} %bitcast.147, f32[64,1,128]{2,1,0:T(1,128)S(1)} %get-tuple-element.270, f32[64,1,128]{2,1,0:T(1,128)S(1)} %get-tuple-element.271, f32[64,3,128]{2,1,0:T(4,128)S(1)} %fusion.47, ...), kind=kOutput, calls=%fused_computation.4.clone.1 | convolution fusion | flops 63037440 | bytes 4621056 | tf_op jit(solution)/shard_map/while/body/eval_jaxpr/scp,spq->scq/dot_general | solution.py:95
  146.7 7.4 %fusion.48 = f32[8,64,5,128]{3,2,1,0:T(8,128)} fusion(f32[8,64,5,128]{3,2,1,0:T(8,128)} %get-tuple-element.287, s32[]{:T(128)} %get-tuple-element.284, f32[64,128,128]{1,2,0:T(8,128)S(1)} %bitcast.147, f32[64,1,128]{2,1,0:T(1,128)S(1)} %get-tuple-element.270, f32[64,1,128]{2,1,0:T(1,128)S(1)} %get-tuple-element.271, f32[64,3,128]{2,1,0:T(4,128)S(1)} %fusion.47, ...), kind=kOutput, calls=%fused_computation.4.clone.1 | convolution fusion | flops 63037440 | bytes 4621056 | tf_op jit(solution)/shard_map/while/body/eval_jaxpr/scp,spq->scq/dot_general | solution.py:95
  163.7 7.4 %fusion.48 = f32[8,64,5,128]{3,2,1,0:T(8,128)} fusion(f32[8,64,5,128]{3,2,1,0:T(8,128)} %get-tuple-element.287, s32[]{:T(128)} %get-tuple-element.284, f32[64,128,128]{1,2,0:T(8,128)S(1)} %bitcast.147, f32[64,1,128]{2,1,0:T(1,128)S(1)} %get-tuple-element.270, f32[64,1,128]{2,1,0:T(1,128)S(1)} %get-tuple-element.271, f32[64,3,128]{2,1,0:T(4,128)S(1)} %fusion.47, ...), kind=kOutput, calls=%fused_computation.4.clone.1 | convolution fusion | flops 63037440 | bytes 4621056 | tf_op jit(solution)/shard_map/while/body/eval_jaxpr/scp,spq->scq/dot_general | solution.py:95
  180.6 7.4 %fusion.48 = f32[8,64,5,128]{3,2,1,0:T(8,128)} fusion(f32[8,64,5,128]{3,2,1,0:T(8,128)} %get-tuple-element.287, s32[]{:T(128)} %get-tuple-element.284, f32[64,128,128]{1,2,0:T(8,128)S(1)} %bitcast.147, f32[64,1,128]{2,1,0:T(1,128)S(1)} %get-tuple-element.270, f32[64,1,128]{2,1,0:T(1,128)S(1)} %get-tuple-element.271, f32[64,3,128]{2,1,0:T(4,128)S(1)} %fusion.47, ...), kind=kOutput, calls=%fused_computation.4.clone.1 | convolution fusion | flops 63037440 | bytes 4621056 | tf_op jit(solution)/shard_map/while/body/eval_jaxpr/scp,spq->scq/dot_general | solution.py:95
  197.6 7.4 %fusion.48 = f32[8,64,5,128]{3,2,1,0:T(8,128)} fusion(f32[8,64,5,128]{3,2,1,0:T(8,128)} %get-tuple-element.287, s32[]{:T(128)} %get-tuple-element.284, f32[64,128,128]{1,2,0:T(8,128)S(1)} %bitcast.147, f32[64,1,128]{2,1,0:T(1,128)S(1)} %get-tuple-element.270, f32[64,1,128]{2,1,0:T(1,128)S(1)} %get-tuple-element.271, f32[64,3,128]{2,1,0:T(4,128)S(1)} %fusion.47, ...), kind=kOutput, calls=%fused_computation.4.clone.1 | convolution fusion | flops 63037440 | bytes 4621056 | tf_op jit(solution)/shard_map/while/body/eval_jaxpr/scp,spq->scq/dot_general | solution.py:95
  214.6 7.4 %fusion.48 = f32[8,64,5,128]{3,2,1,0:T(8,128)} fusion(f32[8,64,5,128]{3,2,1,0:T(8,128)} %get-tuple-element.287, s32[]{:T(128)} %get-tuple-element.284, f32[64,128,128]{1,2,0:T(8,128)S(1)} %bitcast.147, f32[64,1,128]{2,1,0:T(1,128)S(1)} %get-tuple-element.270, f32[64,1,128]{2,1,0:T(1,128)S(1)} %get-tuple-element.271, f32[64,3,128]{2,1,0:T(4,128)S(1)} %fusion.47, ...), kind=kOutput, calls=%fused_computation.4.clone.1 | convolution fusion | flops 63037440 | bytes 4621056 | tf_op jit(solution)/shard_map/while/body/eval_jaxpr/scp,spq->scq/dot_general | solution.py:95
  226.4 5.1 %all-to-all-start.2 = ((f32[128,4,5,128]{3,1,2,0:T(4,128)}), f32[128,4,5,128]{3,1,2,0:T(4,128)S(1)}, u32[]{:S(2)}, u32[]{:S(2)}) async-start(f32[128,4,5,128]{3,1,2,0:T(4,128)} %copy.110), calls=%async_computation.2 | async-start | bytes 2621440 | tf_op jit(solution)/shard_map/all_to_all | solution.py:137
  233.0 4.2 %collective-permute-start.3 = (f32[5,16,1,256]{3,2,1,0:T(1,128)S(1)}, f32[5,16,1,256]{3,2,1,0:T(1,128)S(1)}, u32[]{:S(2)}, u32[]{:S(2)}) collective-permute-start(f32[5,16,1,256]{3,2,1,0:T(1,128)S(1)} %get-tuple-element.166), channel_id=1, source_target_pairs={{0,1},{1,2},{2,3},{3,4},{4,5},{5,6},{6,7},{7,8},{8,9},{9,10},{10,1... | collective-permute-start | bytes 245768 | tf_op jit(solution)/shard_map/ppermute | solution.py:28
  237.2 4.0 %collective-permute-start.1 = (f32[5,1,16,256]{3,2,1,0:T(8,128)S(1)}, f32[5,1,16,256]{3,2,1,0:T(8,128)S(1)}, u32[]{:S(2)}, u32[]{:S(2)}) collective-permute-start(f32[5,1,16,256]{3,2,1,0:T(8,128)S(1)} %get-tuple-element.169), channel_id=1, source_target_pairs={{0,16},{16,32},{32,48},{48,64},{64,80},{80,96},{96,112},{1,17},{17... | collective-permute-start | bytes 245768 | tf_op jit(solution)/shard_map/ppermute | solution.py:28
  243.9 5.8 %collective-permute-done.2 = f32[5,16,1,256]{3,2,1,0:T(1,128)S(1)} collective-permute-done((f32[5,16,1,256]{3,2,1,0:T(1,128)S(1)}, f32[5,16,1,256]{3,2,1,0:T(1,128)S(1)}, u32[]{:S(2)}, u32[]{:S(2)}) %collective-permute-start.2) | collective-permute-done | bytes 81952 | tf_op jit(solution)/shard_map/ppermute | solution.py:29
  257.2 35.9 %scatter_fusion = f32[512,5,128]{2,1,0:T(8,128)S(1)} fusion(f32[512,5,128]{2,1,0:T(8,128)S(1)} %broadcast_in_dim.33, s32[512]{0:T(512)S(1)} %reshape.260, f32[512,5,128]{2,1,0:T(8,128)} %copy.112), kind=kCustom, calls=%fused_computation.1 | custom fusion | flops 327680 | bytes 3934208 | tf_op jit(solution)/shard_map/scatter-add | solution.py:138
  296.1 4.3 %div.48 = f32[4,4,32,5,4,4,8]{2,1,0,6,5,4,3:T(4,128)} reshape(f32[512,5,128]{0,2,1:T(8,128)S(1)} %copy.114) | data formatting | bytes 2621440 | tf_op jit(solution)/shard_map/div | solution.py:142
  300.4 13.0 %copy.115 = f32[5,4,4,4,4,32,8]{6,5,4,3,2,1,0:T(8,128)} copy(f32[5,4,4,4,4,32,8]{5,3,1,6,4,2,0:T(4,128)} %bitcast.149) | data formatting | bytes 2621440 | tf_op jit(solution)/shard_map/div | solution.py:142
  313.4 16.6 %div.50 = f32[5,16,16,256]{3,2,1,0:T(8,128)} reshape(f32[5,4,4,4,4,32,8]{6,5,4,3,2,1,0:T(8,128)} %copy.115) | data formatting | bytes 2621440 | tf_op jit(solution)/shard_map/div | solution.py:142
  330.0 5.0 %fusion.27 = f32[5,16,16,256]{3,2,1,0:T(8,128)} fusion(f32[5,16,16,256]{3,2,1,0:T(8,128)} %div.50, f32[5,16,16,256]{3,2,1,0:T(8,128)S(1)} %copy-done, f32[5,18,18,258]{3,2,1,0:T(8,128)} %select_maximum_fusion, f32[5,18,16,256]{3,2,1,0:T(8,128)S(1)} %copy-done.2, f32[5,18,1,256]{3,2,1,0:T(1,128)S(1)} %copy-done.5, f32[5,18,1,256]{3,2,1,0:T(1,128)S(1)} %pad.11, ...), kind=kLoop, calls=%fused_computation.80 | loop fusion | flops 4587520 | bytes 8376320 | tf_op jit(solution)/shard_map/add | solution.py:142
  (225 shorter events, 106.9 us)
Async XLA Ops:
  2.0 47.6 %all-to-all-start = ((s32[128,1,4]{2,1,0:T(1,128)}), s32[128,1,4]{2,1,0:T(1,128)S(1)}, u32[]{:S(2)}, u32[]{:S(2)}) async-start(s32[128,1,4]{2,1,0:T(1,128)} %bitcast.18), calls=%async_computation | async-start | bytes 131072 | tf_op jit(solution)/shard_map/all_to_all | solution.py:132
  55.4 10.3 %copy-start.12 = (s32[1,1,128]{2,1,0:T(1,128)S(1)}, s32[1,1,128]{2,1,0:T(1,128)}, u32[]{:S(2)}) copy-start(s32[1,1,128]{2,1,0:T(1,128)} %param.15) | copy-start | bytes 1540
  55.4 11.3 %copy-start.6 = (f32[1,1,128,4,3,128]{5,3,4,2,1,0:T(4,128)S(1)}, f32[1,1,128,4,3,128]{5,3,4,2,1,0:T(4,128)}, u32[]{:S(2)}) copy-start(f32[1,1,128,4,3,128]{5,3,4,2,1,0:T(4,128)} %param.10) | copy-start | bytes 2359300
  55.4 31.0 %all-to-all-start.1 = ((f32[128,4,5,128]{3,1,2,0:T(4,128)}), f32[128,4,5,128]{3,1,2,0:T(4,128)S(1)}, u32[]{:S(2)}, u32[]{:S(2)}) async-start(f32[128,4,5,128]{3,1,2,0:T(4,128)} %copy.101), calls=%async_computation.1 | async-start | bytes 2621440 | tf_op jit(solution)/shard_map/all_to_all | solution.py:133
  66.7 1.6 copy-start.7
  226.4 5.1 %copy-start = (f32[5,16,16,256]{3,2,1,0:T(8,128)S(1)}, f32[5,16,16,256]{3,2,1,0:T(8,128)}, u32[]{:S(2)}) copy-start(f32[5,16,16,256]{3,2,1,0:T(8,128)} %param.9) | copy-start | bytes 3932164
  226.4 28.2 %all-to-all-start.2 = ((f32[128,4,5,128]{3,1,2,0:T(4,128)}), f32[128,4,5,128]{3,1,2,0:T(4,128)S(1)}, u32[]{:S(2)}, u32[]{:S(2)}) async-start(f32[128,4,5,128]{3,1,2,0:T(4,128)} %copy.110), calls=%async_computation.2 | async-start | bytes 2621440 | tf_op jit(solution)/shard_map/all_to_all | solution.py:137
  231.7 18.1 %collective-permute-start.2 = (f32[5,16,1,256]{3,2,1,0:T(1,128)S(1)}, f32[5,16,1,256]{3,2,1,0:T(1,128)S(1)}, u32[]{:S(2)}, u32[]{:S(2)}) collective-permute-start(f32[5,16,1,256]{3,2,1,0:T(1,128)S(1)} %get-tuple-element.167), channel_id=1, source_target_pairs={{1,0},{2,1},{3,2},{4,3},{5,4},{6,5},{7,6},{8,7},{9,8},{10,9},{11,1... | collective-permute-start | bytes 245768 | tf_op jit(solution)/shard_map/ppermute | solution.py:29
  233.0 16.8 %collective-permute-start.3 = (f32[5,16,1,256]{3,2,1,0:T(1,128)S(1)}, f32[5,16,1,256]{3,2,1,0:T(1,128)S(1)}, u32[]{:S(2)}, u32[]{:S(2)}) collective-permute-start(f32[5,16,1,256]{3,2,1,0:T(1,128)S(1)} %get-tuple-element.166), channel_id=1, source_target_pairs={{0,1},{1,2},{2,3},{3,4},{4,5},{5,6},{6,7},{7,8},{8,9},{9,10},{10,1... | collective-permute-start | bytes 245768 | tf_op jit(solution)/shard_map/ppermute | solution.py:28
  237.2 12.7 %collective-permute-start.1 = (f32[5,1,16,256]{3,2,1,0:T(8,128)S(1)}, f32[5,1,16,256]{3,2,1,0:T(8,128)S(1)}, u32[]{:S(2)}, u32[]{:S(2)}) collective-permute-start(f32[5,1,16,256]{3,2,1,0:T(8,128)S(1)} %get-tuple-element.169), channel_id=1, source_target_pairs={{0,16},{16,32},{32,48},{48,64},{64,80},{80,96},{96,112},{1,17},{17... | collective-permute-start | bytes 245768 | tf_op jit(solution)/shard_map/ppermute | solution.py:28
  241.2 8.9 %collective-permute-start = (f32[5,1,16,256]{3,2,1,0:T(8,128)S(1)}, f32[5,1,16,256]{3,2,1,0:T(8,128)S(1)}, u32[]{:S(2)}, u32[]{:S(2)}) collective-permute-start(f32[5,1,16,256]{3,2,1,0:T(8,128)S(1)} %get-tuple-element.168), channel_id=1, source_target_pairs={{16,0},{32,16},{48,32},{64,48},{80,64},{96,80},{112,96},{17,1},{33... | collective-permute-start | bytes 245768 | tf_op jit(solution)/shard_map/ppermute | solution.py:29
  249.9 3.7 %copy-start.4 = (f32[5,18,1,256]{3,2,1,0:T(1,128)}, f32[5,18,1,256]{3,2,1,0:T(1,128)S(1)}, u32[]{:S(2)}) copy-start(f32[5,18,1,256]{3,2,1,0:T(1,128)S(1)} %pad.12) | copy-start | bytes 276484
  249.9 3.6 %copy-start.8 = (f32[5,1,16,256]{3,2,1,0:T(8,128)}, f32[5,1,16,256]{3,2,1,0:T(8,128)S(1)}, u32[]{:S(2)}) copy-start(f32[5,1,16,256]{3,2,1,0:T(8,128)S(1)} %collective-permute-done.1) | copy-start | bytes 245764
  250.0 3.5 %copy-start.10 = (f32[5,1,16,256]{3,2,1,0:T(8,128)}, f32[5,1,16,256]{3,2,1,0:T(8,128)S(1)}, u32[]{:S(2)}) copy-start(f32[5,1,16,256]{3,2,1,0:T(8,128)S(1)} %collective-permute-done) | copy-start | bytes 245764
  250.1 3.5 %copy-start.1 = (f32[5,18,16,256]{3,2,1,0:T(8,128)}, f32[5,18,16,256]{3,2,1,0:T(8,128)S(1)}, u32[]{:S(2)}) copy-start(f32[5,18,16,256]{3,2,1,0:T(8,128)S(1)} %constant_dynamic-update-slice_fusion) | copy-start | bytes 4423684
  250.1 3.5 %copy-start.3 = (f32[8,64,3,128]{3,2,1,0:T(4,128)S(1)}, f32[8,64,3,128]{3,2,1,0:T(4,128)}, u32[]{:S(2)}) copy-start(f32[8,64,3,128]{3,2,1,0:T(4,128)} %get-tuple-element.58) | copy-start | bytes 2359300
  313.4 16.6 %copy-start.2 = (f32[5,18,16,256]{3,2,1,0:T(8,128)S(1)}, f32[5,18,16,256]{3,2,1,0:T(8,128)}, u32[]{:S(2)}) copy-start(f32[5,18,16,256]{3,2,1,0:T(8,128)} %copy-done.1) | copy-start | bytes 4423684
  313.4 16.6 %copy-start.5 = (f32[5,18,1,256]{3,2,1,0:T(1,128)S(1)}, f32[5,18,1,256]{3,2,1,0:T(1,128)}, u32[]{:S(2)}) copy-start(f32[5,18,1,256]{3,2,1,0:T(1,128)} %copy-done.4) | copy-start | bytes 276484
  313.4 16.6 %copy-start.9 = (f32[5,1,16,256]{3,2,1,0:T(8,128)S(1)}, f32[5,1,16,256]{3,2,1,0:T(8,128)}, u32[]{:S(2)}) copy-start(f32[5,1,16,256]{3,2,1,0:T(8,128)} %copy-done.8) | copy-start | bytes 245764
  313.4 16.6 %copy-start.11 = (f32[5,1,16,256]{3,2,1,0:T(8,128)S(1)}, f32[5,1,16,256]{3,2,1,0:T(8,128)}, u32[]{:S(2)}) copy-start(f32[5,1,16,256]{3,2,1,0:T(8,128)} %copy-done.10) | copy-start | bytes 245764
where the time goes:
time: 340 us; the launch traced here: 335 us
  local copies, waits for them, and re-layouts  105 us (31%)
  matrix products  88.4 us (26%)
  other arithmetic  78.6 us (23%)
  starting transfers between devices  37.7 us (11%)
  waiting for transfers between devices  23 us (7%)
    dot_general x8, matrix products, parcel_update(): jnp.einsum('scp,spq->scq', source, stencil, precision=lax.Precision.HIGHEST)  59 us
    scatter-add x1, other arithmetic, shards(): jax.ops.segment_sum(arrived.reshape(slot_total, fields, -1), wanted.resha...  35.9 us
    div x4, local copies, waits for them, and re-layouts, shards(): gas_next = gas_state + DIFFUSION * diffused + source_field / CELL_MASS  35.6 us
    dot_general x8, matrix products, parcel_update(): jnp.einsum('scq,spq->scp', tile_data, stencil, precision=lax.Precision.HI...  29.4 us
    all_to_all x1, waiting for transfers between devices, shards(): lax.all_to_all(table[wanted], ('gx', 'yz'), split_axis=0, concat_axis=0,...  17.2 us
    reshape x1, local copies, waits for them, and re-layouts, split_tiles(): block.reshape(fields, extent_x // TILE_X, TILE_X, extent_y // TILE_Y, TIL...  14.5 us
    transpose x1, local copies, waits for them, and re-layouts, split_tiles(): grid = grid.transpose(1, 3, 5, 0, 2, 4, 6)  14.1 us
    dynamic_update_slice x16, other arithmetic, in_groups(): lax.map(process, tuple((grouped(member) for member in (tile_data, velocit...  11.9 us
  transfers between devices with their start and end apart: 7, of which 2 were waited for; matrix products, arithmetic and copies ran while one was open for 14% of the time, Pallas kernels for 0%

commit v1 on v0

v1 whole, which is shorter than its diff:
```python
import functools

import jax
import jax.numpy as jnp
from jax import lax
from jax.experimental import pallas as pl
from jax.experimental.pallas import tpu as pltpu
from jax.sharding import PartitionSpec as P

F32 = jnp.float32
BF16 = jnp.bfloat16
I32 = jnp.int32

DIFFUSION = 0.1
CELL_MASS = 4.0
DRAG_RATE = 0.5
EVAPORATION = 0.3
LATENT_HEAT = 2.0

CORNERS = tuple((u, v, w) for u in (0, 1) for v in (0, 1) for w in (0, 1))
SHIFTS = tuple(u * 32 + v * 8 + w for u, v, w in CORNERS)


def lanes():
    return lax.broadcasted_iota(I32, (8, 128), 1)


def rows():
    return lax.broadcasted_iota(I32, (8, 128), 0)


def chunk_swaps():
    row, lane = rows(), lanes()
    half, chunk, rest = lane // 64, (lane // 8) % 8, lane % 8
    first = half * 64 + ((chunk - row) % 8) * 8 + rest
    second = (chunk - row) % 8
    third = half * 64 + ((chunk + row) % 8) * 8 + rest
    return first, second, third


def transpose_chunks(block, swaps):
    first, second, third = swaps
    block = jnp.take_along_axis(block, first, axis=1)
    block = jnp.take_along_axis(block, second, axis=0)
    return jnp.take_along_axis(block, third, axis=1)


def swap_halves(a, b, axis):
    size = a.shape[axis] // 2
    low = (lanes() < 64) if axis == 1 else (rows() < 4)
    crossed = pltpu.roll(jnp.where(low, b, a), size, axis)
    return jnp.where(low, a, crossed), jnp.where(low, crossed, b)


def grid_to_tiles(blocks, swaps):
    pairs = [swap_halves(blocks[k], blocks[2 + k], 1) for k in (0, 1)]
    out = []
    for z in (0, 1):
        halves = swap_halves(pairs[0][z], pairs[1][z], 0)
        out.append([transpose_chunks(one, swaps) for one in halves])
    return out


def tiles_to_grid(tiles, swaps):
    pairs = []
    for z in (0, 1):
        a, b = (transpose_chunks(one, swaps) for one in tiles[z])
        pairs.append(swap_halves(a, b, 0))
    blocks = [None] * 4
    for k in (0, 1):
        blocks[k], blocks[2 + k] = swap_halves(pairs[0][k], pairs[1][k], 1)
    return blocks


def table_kernel(gas_ref, table_ref):
    swaps = chunk_swaps()

    def step(n, carry):
        a, yo = n // 2, n % 2
        y0 = pl.multiple_of(yo * 8, 8)
        for h in (0, 1):
            for f in range(4):
                blocks = []
                for u in range(4):
                    part = gas_ref[f, a * 4 + u, pl.ds(y0, 8), pl.ds(h * 128, 128)]
                    if f == 3:
                        part = part - gas_ref[4, a * 4 + u, pl.ds(y0, 8), pl.ds(h * 128, 128)]
                    blocks.append(part)
                tiles = grid_to_tiles(blocks, swaps)
                for z in (0, 1):
                    for bh in (0, 1):
                        t0 = (a * 4 + yo * 2 + bh) * 32 + (h * 2 + z) * 8
                        table_ref[pl.ds(t0 * 4 + f, 8, stride=4), :] = tiles[z][bh]
        return carry

    lax.fori_loop(0, 8, step, 0)


def gather_kernel(index_ref, table_ref, out_ref):
    def step(n, carry):
        for k in range(16):
            s = n * 16 + k
            out_ref[s] = table_ref[index_ref[s]]
        return carry

    lax.fori_loop(0, out_ref.shape[0] // 16, step, 0)


def split_three(ref, g):
    low = rows() < 4
    v0, v1, v2 = (ref[pl.ds(pl.multiple_of(g * 24 + 8 * n, 8), 8), :] for n in range(3))
    middle = pltpu.roll(jnp.where(low, v2, v0), 4, 0)
    return jnp.where(low, v0, v1), middle, jnp.where(low, v1, v2)


def join_three(ref, g, f0, f1, f2):
    low = rows() < 4
    middle = pltpu.roll(f1, 4, 0)
    out = (jnp.where(low, f0, middle), jnp.where(low, f2, f0), jnp.where(low, middle, f2))
    for n in range(3):
        ref[pl.ds(pl.multiple_of(g * 24 + 8 * n, 8), 8), :] = out[n]


def parcels(g, count_ref, tiles_ref, speed_ref, mass_ref, offset_ref, cell_ref, speed_out, mass_out, lhs_ref, q_ref):
    low = rows() < 4
    cx, cy, cz = split_three(cell_ref, g)
    ox, oy, oz = split_three(offset_ref, g)
    speed = split_three(speed_ref, g)
    mass = mass_ref[pl.ds(pl.multiple_of(g * 8, 8), 8), :]
    q = cx * 32 + cy * 8 + cz
    wx, wy, wz = ((1.0 - o, o) for o in (ox, oy, oz))
    weights = []
    for u in (0, 1):
        for v in (0, 1):
            both = wx[u] * wy[v]
            weights += [both * wz[0], both * wz[1]]
    index = [q + shift for shift in SHIFTS]
    sampled = []
    for f in range(4):
        tile = tiles_ref[pl.ds(g * 32 + f, 8, stride=4), :]
        total = None
        for c in range(8):
            term = jnp.take_along_axis(tile, index[c], axis=1) * weights[c]
            total = term if total is None else total + term
        sampled.append(total)
    log_radius = jnp.log(mass) * (1.0 / 3.0)
    inverse_radius = jnp.exp(-log_radius)
    drag = DRAG_RATE * inverse_radius * inverse_radius
    live = (rows() % 4) < jnp.where(low, count_ref[2 * g], count_ref[2 * g + 1])
    scale = 1.0 / (1.0 + drag)
    gap = sampled[3]
    softplus = jnp.maximum(gap, 0.0) + jnp.log(1.0 + jnp.exp(-jnp.abs(gap)))
    mass_new = mass / (1.0 + EVAPORATION * softplus * inverse_radius)
    mass_new = jnp.where(live, mass_new, mass)
    vapour = mass - mass_new
    speed_new, source = [], []
    for f in range(3):
        moved = jnp.where(live, (speed[f] + drag * sampled[f]) * scale, speed[f])
        speed_new.append(moved)
        source.append(mass * (speed[f] - moved) + vapour * moved)
    source.append(vapour)
    join_three(speed_out, g, *speed_new)
    mass_out[pl.ds(pl.multiple_of(g * 8, 8), 8), :] = mass_new
    for f in range(4):
        value = jnp.where(live, source[f], 0.0)
        for c in range(8):
            lhs_ref[pl.ds(c * 32 + f, 8, stride=4), :] = value * weights[c]
    q_ref[...] = q


def deposits(g, lhs_ref, q_ref, out_ref):
    entry = lax.broadcasted_iota(I32, (128, 128), 0)
    first = lax.broadcasted_iota(I32, (64, 128), 0) % 8 < 4
    keep = jnp.where(first, 1.0, 0.0).astype(BF16)
    drop = jnp.where(first, 0.0, 1.0).astype(BF16)
    for j in range(4):
        left = jnp.concatenate([lhs_ref[pl.ds(c * 32 + j * 8, 8), :] for c in range(8)], axis=0)
        high = left.astype(BF16)
        rest = (left - high.astype(F32)).astype(BF16)
        left = jnp.concatenate(
            [
                jnp.concatenate([high * keep, high * drop], axis=1),
                jnp.concatenate([rest * keep, rest * drop], axis=1),
            ],
            axis=0,
        )
        hits = []
        for k in (0, 1):
            at = jnp.broadcast_to(q_ref[pl.ds(2 * j + k, 1), :], (128, 128))
            hits.append(jnp.where(at == entry, 1.0, 0.0).astype(BF16))
        right = jnp.concatenate(hits, axis=1)
        both = lax.dot_general(left, right, (((1,), (1,)), ((), ())), preferred_element_type=F32)
        both = both[:64] + both[64:]
        total = both[:8]
        for c in range(1, 8):
            total = total + pltpu.roll(both[c * 8 : c * 8 + 8], SHIFTS[c], 1)
        out_ref[pl.ds(pl.multiple_of(g * 32 + j * 8, 8), 8), :] = total


def parcel_kernel(count_ref, tiles_ref, speed_ref, mass_ref, offset_ref, cell_ref, speed_out, mass_out, out_ref, lhs_ref, q_ref):
    groups = mass_ref.shape[0] // 8

    def first(g):
        parcels(g, count_ref, tiles_ref, speed_ref, mass_ref, offset_ref, cell_ref, speed_out, mass_out, lhs_ref, q_ref)

    def step(g, carry):
        deposits(g - 1, lhs_ref, q_ref, out_ref)
        first(g)
        return carry

    first(0)
    lax.fori_loop(1, groups, step, 0)
    deposits(groups - 1, lhs_ref, q_ref, out_ref)


def spread(plane_ref, f, x, xs, halos):
    xlo, xhi, ylo, yhi = halos
    value = plane_ref[f, x]
    row = lax.broadcasted_iota(I32, value.shape, 0)
    lane = lax.broadcasted_iota(I32, value.shape, 1)
    ny, nz = value.shape
    below = xlo[f] if x == 0 else plane_ref[f, x - 1]
    above = xhi[f] if x == xs - 1 else plane_ref[f, x + 1]
    total = below + above
    total = total + jnp.where(row == 0, ylo[f, x : x + 1, :], pltpu.roll(value, 1, 0))
    total = total + jnp.where(row == ny - 1, yhi[f, x : x + 1, :], pltpu.roll(value, ny - 1, 0))
    total = total + jnp.where(lane == 0, 0.0, pltpu.roll(value, 1, 1))
    total = total + jnp.where(lane == nz - 1, 0.0, pltpu.roll(value, nz - 1, 1))
    return value + DIFFUSION * (total - 6.0 * value)


def diffuse_kernel(gas_ref, xlo, xhi, ylo, yhi, out_ref):
    xs = gas_ref.shape[1]

    def step(f, carry):
        for x in range(xs):
            out_ref[f, x] = spread(gas_ref, f, x, xs, (xlo, xhi, ylo, yhi))
        return carry

    lax.fori_loop(0, gas_ref.shape[0], step, 0)


def scatter_kernel(index_ref, arrived_ref, *sum_refs):
    for ref in sum_refs:
        ref[...] = jnp.zeros_like(ref)

    def step(n, carry):
        for k in range(4):
            for m in range(4):
                s = n * 16 + k * 4 + m
                t = index_ref[s]
                sum_refs[m][t] += arrived_ref[s]
        return carry

    lax.fori_loop(0, arrived_ref.shape[0] // 16, step, 0)


def join_kernel(base_ref, s0, s1, s2, s3, out_ref):
    swaps = chunk_swaps()

    def step(n, carry):
        a, yo = n // 2, n % 2
        y0 = pl.multiple_of(yo * 8, 8)
        for h in (0, 1):
            for f in range(4):
                tiles = []
                for z in (0, 1):
                    tiles.append([])
                    for bh in (0, 1):
                        t0 = (a * 4 + yo * 2 + bh) * 32 + (h * 2 + z) * 8
                        at = pl.ds(t0 * 4 + f, 8, stride=4)
                        tiles[z].append((s0[at, :] + s1[at, :]) + (s2[at, :] + s3[at, :]))
                blocks = tiles_to_grid(tiles, swaps)
                for u in range(4):
                    at = (a * 4 + u, pl.ds(y0, 8), pl.ds(h * 128, 128))
                    add = blocks[u] * (1.0 / CELL_MASS)
                    if f < 3:
                        out_ref[f, *at] = base_ref[f, *at] + add
                    else:
                        out_ref[3, *at] = base_ref[3, *at] - LATENT_HEAT * add
                        out_ref[4, *at] = base_ref[4, *at] + add
        return carry

    lax.fori_loop(0, 8, step, 0)


VMEM = pl.BlockSpec(memory_space=pltpu.VMEM)
SMEM = pl.BlockSpec(memory_space=pltpu.SMEM)


def call(kernel, name, out, in_specs, scratch=()):
    return pl.pallas_call(
        kernel,
        name=name,
        out_shape=out,
        in_specs=in_specs,
        out_specs=jax.tree.map(lambda _: VMEM, out),
        scratch_shapes=scratch,
        compiler_params=pltpu.CompilerParams(vmem_limit_bytes=48 * 1024 * 1024),
    )


def array(*shape):
    return jax.ShapeDtypeStruct(shape, F32)


def shards(gas_state, parcel_speed, parcel_mass, offsets, cell_base, block_tile, block_count):
    fields, xs, ys, zs = gas_state.shape
    devices, capacity = block_tile.shape[2:]
    slots = devices * capacity
    tiles = xs * ys * zs // 128

    def three(value):
        value = value.reshape(devices, capacity, 3, 128).transpose(0, 2, 1, 3)
        return value.reshape(slots * 3, 128)

    index = block_tile.reshape(devices, capacity)
    wanted = lax.all_to_all(index, ("gx", "yz"), split_axis=0, concat_axis=0, tiled=True).reshape(slots)
    table = call(table_kernel, "table", array(tiles * 4, 128), [VMEM])(gas_state)

    def edges(axis, dim):
        count, length = lax.axis_size(axis), gas_state.shape[dim]
        up = [(i, i + 1) for i in range(count - 1)]
        last = lax.slice_in_dim(gas_state, length - 1, length, axis=dim)
        initial = lax.slice_in_dim(gas_state, 0, 1, axis=dim)
        return (
            jnp.squeeze(lax.ppermute(last, axis, up), dim),
            jnp.squeeze(lax.ppermute(initial, axis, [(b, a) for a, b in up]), dim),
        )

    halos = edges("gx", 1) + edges("yz", 2)
    send = call(gather_kernel, "gather", array(slots, 4, 128), [SMEM, VMEM])(wanted, table.reshape(tiles, 4, 128))
    fetched = lax.all_to_all(send, ("gx", "yz"), split_axis=0, concat_axis=0, tiled=True)
    base = call(diffuse_kernel, "diffuse", array(*gas_state.shape), [VMEM] * 5)(gas_state, *halos)
    speed_next, mass_next, deposit = call(
        parcel_kernel,
        "parcels",
        (array(slots * 3, 128), array(slots, 128), array(slots * 4, 128)),
        [SMEM] + [VMEM] * 5,
        [pltpu.VMEM((256, 128), F32), pltpu.VMEM((8, 128), I32)],
    )(
        block_count.reshape(devices),
        fetched.reshape(slots * 4, 128),
        three(parcel_speed),
        parcel_mass.reshape(slots, 128),
        three(offsets),
        three(cell_base),
    )
    arrived = lax.all_to_all(deposit.reshape(slots, 4, 128), ("gx", "yz"), split_axis=0, concat_axis=0, tiled=True)
    sums = call(scatter_kernel, "scatter", (array(tiles, 4, 128),) * 4, [SMEM, VMEM])(wanted, arrived)
    gas_next = call(join_kernel, "join", array(*gas_state.shape), [VMEM] * 5)(
        base, *(one.reshape(tiles * 4, 128) for one in sums)
    )
    speed_next = speed_next.reshape(devices, 3, capacity, 128).transpose(0, 2, 1, 3)
    return gas_next, speed_next.reshape(parcel_speed.shape), mass_next.reshape(parcel_mass.shape)


def solution(mesh):
    in_specs = (
        P(None, "gx", "yz", None),
        P("gx", "yz", None, None, None, None),
        P("gx", "yz", None, None, None),
        P("gx", "yz", None, None, None, None),
        P("gx", "yz", None, None, None, None),
        P("gx", "yz", None, None),
        P("gx", "yz", None),
    )
    out_specs = (
        P(None, "gx", "yz", None),
        P("gx", "yz", None, None, None, None),
        P("gx", "yz", None, None, None),
    )
    return jax.shard_map(shards, mesh=mesh, in_specs=in_specs, out_specs=out_specs, check_vma=False)
```

time: 340 us -> 103 us (0.30); the launches traced: 335 us -> 102 us
  local copies, waits for them, and re-layouts: 105 us -> 3.52 us
  matrix products: 88.4 us -> 0 us
  other arithmetic: 78.6 us -> 0.81 us
  Pallas kernels: 0 us -> 33.3 us
  blocking collectives: 0 us -> 23 us
  waiting for transfers between devices: 23 us -> 12.8 us
  starting transfers between devices: 37.7 us -> 28 us
    dot_general x16 -> x0, matrix products: 88.4 us -> none  [the longest x8 59 us: parcel_update(): jnp.einsum('scp,spq->scq', source, stencil, precision=lax.Precision.HIGHEST)]
    scatter-add x1 -> x0, other arithmetic: 35.9 us -> none  [shards(): jax.ops.segment_sum(arrived.reshape(slot_total, fields, -1), wanted.resha...]
    div x4 -> x0, local copies, waits for them, and re-layouts: 35.6 us -> none  [shards(): gas_next = gas_state + DIFFUSION * diffused + source_field / CELL_MASS]
    pallas_call x0 -> x6, Pallas kernels: none -> 33.3 us  [the longest x1 23.3 us: shards(): call(parcel_kernel, 'parcels', (array(slots * 3, 128), array(slots, 128),...]
    reshape x5 -> x1, local copies, waits for them, and re-layouts: 27.1 us -> 0.1 us  [shards(): lax.all_to_all(index, ('gx', 'yz'), split_axis=0, concat_axis=0, tiled=True)]
    all_to_all x0 -> x1, blocking collectives: none -> 23 us  [shards(): lax.all_to_all(send, ('gx', 'yz'), split_axis=0, concat_axis=0, tiled=True)]
    transpose x1 -> x0, local copies, waits for them, and re-layouts: 14.1 us -> none  [split_tiles(): grid = grid.transpose(1, 3, 5, 0, 2, 4, 6)]
    dynamic_update_slice x16 -> x0, other arithmetic: 11.9 us -> none  [in_groups(): lax.map(process, tuple((grouped(member) for member in (tile_data, velocit...]
  transfers between devices with their start and end apart: 7 -> 6, of which waited for: 2 -> 4; matrix products, arithmetic and copies ran while one was open for 14% -> 0% of each run, Pallas kernels for 0% -> 3%
where the time goes in v1:
time: 103 us; the launch traced here: 102 us
  Pallas kernels  33.3 us (32%)
  starting transfers between devices  28 us (27%)
  blocking collectives  23 us (22%)
  waiting for transfers between devices  12.8 us (12%)
  local copies, waits for them, and re-layouts  3.52 us (3%)
    pallas_call x1, Pallas kernels, shards(): call(parcel_kernel, 'parcels', (array(slots * 3, 128), array(slots, 128),...  23.3 us
    all_to_all x1, blocking collectives, shards(): lax.all_to_all(send, ('gx', 'yz'), split_axis=0, concat_axis=0, tiled=True)  23 us
    all_to_all x1, starting transfers between devices, shards(): lax.all_to_all(index, ('gx', 'yz'), split_axis=0, concat_axis=0, tiled=True)  11.5 us
    ppermute x2, starting transfers between devices, edges(): lax.ppermute(last, axis, up)  6.58 us
    all_to_all x1, waiting for transfers between devices, shards(): lax.all_to_all(index, ('gx', 'yz'), split_axis=0, concat_axis=0, tiled=True)  6.12 us
    all_to_all x1, starting transfers between devices, shards(): lax.all_to_all(deposit.reshape(slots, 4, 128), ('gx', 'yz'), split_axis=0...  6.05 us
    ppermute x2, waiting for transfers between devices, edges(): lax.ppermute(initial, axis, [(b, a) for a, b in up])  4.49 us
    ppermute x2, starting transfers between devices, edges(): lax.ppermute(initial, axis, [(b, a) for a, b in up])  3.87 us
  transfers between devices with their start and end apart: 6, of which 4 were waited for; matrix products, arithmetic and copies ran while one was open for 0% of the time, Pallas kernels for 3%

profile of v1, /device:TPU:1, one launch (start us, length us, event | category | flops | bytes accessed | tf_op | source)
XLA Modules:
  0.0 102.3 jit_solution(15660337320235003002)
XLA Ops:
  0.6 1.4 %copy.23 = s32[1,1,128,4]{3,2,1,0:T(8,128)} copy(s32[1,1,128,4]{2,3,1,0:T(4,128)} %param.12) | data formatting | bytes 4096 | tf_op args[5]
  2.0 11.5 %all-to-all-start = ((s32[128,1,4]{2,1,0:T(1,128)}), s32[128,1,4]{2,1,0:T(1,128)S(1)}, u32[]{:S(2)}, u32[]{:S(2)}) async-start(s32[128,1,4]{2,1,0:T(1,128)} %bitcast.4), calls=%async_computation | async-start | bytes 131072 | tf_op jit(solution)/shard_map/all_to_all | solution.py:318
  13.6 1.3 %copy-done = f32[5,16,16,256]{3,2,1,0:T(8,128)S(1)} copy-done((f32[5,16,16,256]{3,2,1,0:T(8,128)S(1)}, f32[5,16,16,256]{3,2,1,0:T(8,128)}, u32[]{:S(2)}) %copy-start) | copy-done | bytes 1310744
  14.9 2.0 %table.1 = f32[2048,128]{1,0:T(8,128)S(1)} custom-call(f32[5,16,16,256]{3,2,1,0:T(8,128)S(1)} %copy-done), custom_call_target="tpu_custom_call" | custom-call | tf_op jit(solution)/shard_map/table/pallas_call | solution.py:319
  16.9 6.1 %all-to-all-done = s32[128,1,4]{2,1,0:T(1,128)S(1)} async-done(((s32[128,1,4]{2,1,0:T(1,128)}), s32[128,1,4]{2,1,0:T(1,128)S(1)}, u32[]{:S(2)}, u32[]{:S(2)}) %all-to-all-start) | async-done | bytes 2080 | tf_op jit(solution)/shard_map/all_to_all | solution.py:318
  23.0 0.5 broadcast.3
  23.5 0.8 reduce.3
  24.3 0.1 reshape.68.index_ref
  24.5 0.0 copy-start.4
  24.5 1.3 %gather.1 = f32[512,4,128]{2,1,0:T(4,128)S(1)} custom-call(s32[512]{0:T(512)S(1)} %reshape.68.index_ref, f32[512,4,128]{2,1,0:T(4,128)S(1)} %bitcast.39), custom_call_target="tpu_custom_call" | custom-call | tf_op jit(solution)/shard_map/gather/pallas_call | solution.py:332
  25.8 23.0 %all_to_all.19 = f32[512,4,128]{2,1,0:T(4,128)S(1)} all-to-all(f32[512,4,128]{2,1,0:T(4,128)S(1)} %gather.1), channel_id=1, replica_groups=mesh['gx'=8,'yz'=16] {'gx','yz'}, dimensions={0} | all-to-all | bytes 2097152 | tf_op jit(solution)/shard_map/all_to_all | solution.py:333
  48.8 23.3 %parcels.1 = (f32[1536,128]{1,0:T(8,128)}, f32[512,128]{1,0:T(8,128)}, f32[2048,128]{1,0:T(8,128)}) custom-call(s32[128]{0:T(128)S(1)} %bitcast.53, f32[2048,128]{1,0:T(8,128)S(1)} %bitcast.40, f32[1536,128]{1,0:T(8,128)S(1)} %bitcast.45, f32[512,128]{1,0:T(8,128)S(1)} %bitcast.48, f32[1536,128]{1,0:T(8,128)S(1)} %bitcast.46, s32[1536,128]{1,0:T(8,128)S(1)} %bitcast.47), custom_call_target="tpu_custom_call" | custom-call | tf_op jit(solution)/shard_map/parcels/pallas_call | solution.py:335
  72.1 6.0 %all-to-all-start.2 = ((f32[512,4,128]{2,1,0:T(4,128)}), f32[512,4,128]{2,1,0:T(4,128)}, u32[]{:S(2)}, u32[]{:S(2)}) async-start(f32[512,4,128]{2,1,0:T(4,128)} %bitcast.18), calls=%async_computation.2 | async-start | bytes 2097152 | tf_op jit(solution)/shard_map/all_to_all | solution.py:349
  78.2 0.1 fusion
  78.3 3.5 %collective-permute-start.2 = (f32[5,16,1,256]{3,1,0,2:T(8,128)S(1)}, f32[5,16,1,256]{3,1,0,2:T(8,128)S(1)}, u32[]{:S(2)}, u32[]{:S(2)}) collective-permute-start(f32[5,16,1,256]{3,1,0,2:T(8,128)S(1)} %copy.26), channel_id=1, source_target_pairs={{0,1},{1,2},{2,3},{3,4},{4,5},{5,6},{6,7},{7,8},{8,9},{9,10},{10,1... | collective-permute-start | bytes 245768 | tf_op jit(solution)/shard_map/ppermute | solution.py:327
  81.9 1.3 %collective-permute-start.3 = (f32[5,16,1,256]{3,1,0,2:T(8,128)S(1)}, f32[5,16,1,256]{3,1,0,2:T(8,128)S(1)}, u32[]{:S(2)}, u32[]{:S(2)}) collective-permute-start(f32[5,16,1,256]{3,1,0,2:T(8,128)S(1)} %copy.27), channel_id=1, source_target_pairs={{1,0},{2,1},{3,2},{4,3},{5,4},{6,5},{7,6},{8,7},{9,8},{10,9},{11,1... | collective-permute-start | bytes 245768 | tf_op jit(solution)/shard_map/ppermute | solution.py:328
  83.2 2.6 %collective-permute-start.1 = (f32[5,1,16,256]{3,2,0,1:T(8,128)S(1)}, f32[5,1,16,256]{3,2,0,1:T(8,128)S(1)}, u32[]{:S(2)}, u32[]{:S(2)}) collective-permute-start(f32[5,1,16,256]{3,2,0,1:T(8,128)S(1)} %get-tuple-element.19), channel_id=1, source_target_pairs={{16,0},{32,16},{48,32},{64,48},{80,64},{96,80},{112,96},{17,1},{33... | collective-permute-start | bytes 245768 | tf_op jit(solution)/shard_map/ppermute | solution.py:328
  85.8 3.1 %collective-permute-start = (f32[5,1,16,256]{3,2,0,1:T(8,128)S(1)}, f32[5,1,16,256]{3,2,0,1:T(8,128)S(1)}, u32[]{:S(2)}, u32[]{:S(2)}) collective-permute-start(f32[5,1,16,256]{3,2,0,1:T(8,128)S(1)} %get-tuple-element.20), channel_id=1, source_target_pairs={{0,16},{16,32},{32,48},{48,64},{64,80},{80,96},{96,112},{1,17},{17... | collective-permute-start | bytes 245768 | tf_op jit(solution)/shard_map/ppermute | solution.py:327
  88.8 0.5 collective-permute-done.2
  89.4 4.5 %collective-permute-done.3 = f32[5,16,1,256]{3,1,0,2:T(8,128)S(1)} collective-permute-done((f32[5,16,1,256]{3,1,0,2:T(8,128)S(1)}, f32[5,16,1,256]{3,1,0,2:T(8,128)S(1)}, u32[]{:S(2)}, u32[]{:S(2)}) %collective-permute-start.3) | collective-permute-done | bytes 81952 | tf_op jit(solution)/shard_map/ppermute | solution.py:328
  93.9 1.1 %diffuse.1.base_ref = f32[5,16,16,256]{3,2,1,0:T(8,128)S(1)} custom-call(f32[5,16,16,256]{3,2,1,0:T(8,128)S(1)} %copy-done.1, f32[5,16,256]{2,1,0:T(8,128)S(1)} %bitcast.52, f32[5,16,256]{2,1,0:T(8,128)S(1)} %bitcast.51, f32[5,16,256]{2,1,0:T(8,128)S(1)} %bitcast.49, f32[5,16,256]{2,1,0:T(8,128)S(1)} %bitcast.50), custom_call_target="tpu_custom_call" | custom-call | tf_op jit(solution)/shard_map/diffuse/pallas_call | solution.py:334
  94.9 1.7 %all-to-all-done.2.arrived_ref = f32[512,4,128]{2,1,0:T(4,128)} async-done(((f32[512,4,128]{2,1,0:T(4,128)}), f32[512,4,128]{2,1,0:T(4,128)}, u32[]{:S(2)}, u32[]{:S(2)}) %all-to-all-start.2) | async-done | bytes 1048608 | tf_op jit(solution)/shard_map/all_to_all | solution.py:349
  96.6 2.5 %scatter.1 = (f32[512,4,128]{2,1,0:T(4,128)S(1)}, f32[512,4,128]{2,1,0:T(4,128)S(1)}, f32[512,4,128]{2,1,0:T(4,128)S(1)}, f32[512,4,128]{2,1,0:T(4,128)S(1)}) custom-call(s32[512]{0:T(512)S(1)} %reshape.68.index_ref, f32[512,4,128]{2,1,0:T(4,128)} %all-to-all-done.2.arrived_ref), custom_call_target="tpu_custom_call" | custom-call | tf_op jit(solution)/shard_map/scatter/pallas_call | solution.py:350
  99.1 3.2 %join.1 = f32[5,16,16,256]{3,2,1,0:T(8,128)} custom-call(f32[5,16,16,256]{3,2,1,0:T(8,128)S(1)} %diffuse.1.base_ref, f32[2048,128]{1,0:T(8,128)S(1)} %bitcast.41, f32[2048,128]{1,0:T(8,128)S(1)} %bitcast.42, f32[2048,128]{1,0:T(8,128)S(1)} %bitcast.43, f32[2048,128]{1,0:T(8,128)S(1)} %bitcast.44), custom_call_target="tpu_custom_call" | custom-call | tf_op jit(solution)/shard_map/join/pallas_call | solution.py:351
  (17 shorter events, 0.1 us)
Async XLA Ops:
  2.0 21.0 %all-to-all-start = ((s32[128,1,4]{2,1,0:T(1,128)}), s32[128,1,4]{2,1,0:T(1,128)S(1)}, u32[]{:S(2)}, u32[]{:S(2)}) async-start(s32[128,1,4]{2,1,0:T(1,128)} %bitcast.4), calls=%async_computation | async-start | bytes 131072 | tf_op jit(solution)/shard_map/all_to_all | solution.py:318
  13.5 1.3 %copy-start = (f32[5,16,16,256]{3,2,1,0:T(8,128)S(1)}, f32[5,16,16,256]{3,2,1,0:T(8,128)}, u32[]{:S(2)}) copy-start(f32[5,16,16,256]{3,2,1,0:T(8,128)} %gas_ref.3) | copy-start | bytes 3932164
  24.5 24.3 %copy-start.4 = (s32[1,1,128,4,3,128]{5,3,4,2,1,0:T(4,128)S(1)}, s32[1,1,128,4,3,128]{5,3,4,2,1,0:T(4,128)}, u32[]{:S(2)}) copy-start(s32[1,1,128,4,3,128]{5,3,4,2,1,0:T(4,128)} %param.11) | copy-start | bytes 2359300
  25.7 23.0 %copy-start.2 = (f32[1,1,128,4,3,128]{5,3,4,2,1,0:T(4,128)S(1)}, f32[1,1,128,4,3,128]{5,3,4,2,1,0:T(4,128)}, u32[]{:S(2)}) copy-start(f32[1,1,128,4,3,128]{5,3,4,2,1,0:T(4,128)} %param.8) | copy-start | bytes 2359300
  25.7 23.0 %copy-start.3 = (f32[1,1,128,4,3,128]{5,3,4,2,1,0:T(4,128)S(1)}, f32[1,1,128,4,3,128]{5,3,4,2,1,0:T(4,128)}, u32[]{:S(2)}) copy-start(f32[1,1,128,4,3,128]{5,3,4,2,1,0:T(4,128)} %param.10) | copy-start | bytes 2359300
  25.8 23.0 %copy-start.5 = (f32[1,1,128,4,128]{4,3,2,1,0:T(4,128)S(1)}, f32[1,1,128,4,128]{4,3,2,1,0:T(4,128)}, u32[]{:S(2)}) copy-start(f32[1,1,128,4,128]{4,3,2,1,0:T(4,128)} %param.9) | copy-start | bytes 786436
  25.8 23.0 %copy-start.6 = (s32[1,1,128]{2,1,0:T(1,128)S(1)}, s32[1,1,128]{2,1,0:T(1,128)}, u32[]{:S(2)}) copy-start(s32[1,1,128]{2,1,0:T(1,128)} %param.13) | copy-start | bytes 1540
  72.1 6.1 %copy-start.1 = (f32[5,16,16,256]{3,2,1,0:T(8,128)S(1)}, f32[5,16,16,256]{3,2,1,0:T(8,128)}, u32[]{:S(2)}) copy-start(f32[5,16,16,256]{3,2,1,0:T(8,128)} %gas_ref.3) | copy-start | bytes 3932164
  72.1 24.5 %all-to-all-start.2 = ((f32[512,4,128]{2,1,0:T(4,128)}), f32[512,4,128]{2,1,0:T(4,128)}, u32[]{:S(2)}, u32[]{:S(2)}) async-start(f32[512,4,128]{2,1,0:T(4,128)} %bitcast.18), calls=%async_computation.2 | async-start | bytes 2097152 | tf_op jit(solution)/shard_map/all_to_all | solution.py:349
  78.3 11.0 %collective-permute-start.2 = (f32[5,16,1,256]{3,1,0,2:T(8,128)S(1)}, f32[5,16,1,256]{3,1,0,2:T(8,128)S(1)}, u32[]{:S(2)}, u32[]{:S(2)}) collective-permute-start(f32[5,16,1,256]{3,1,0,2:T(8,128)S(1)} %copy.26), channel_id=1, source_target_pairs={{0,1},{1,2},{2,3},{3,4},{4,5},{5,6},{6,7},{7,8},{8,9},{9,10},{10,1... | collective-permute-start | bytes 245768 | tf_op jit(solution)/shard_map/ppermute | solution.py:327
  81.9 12.0 %collective-permute-start.3 = (f32[5,16,1,256]{3,1,0,2:T(8,128)S(1)}, f32[5,16,1,256]{3,1,0,2:T(8,128)S(1)}, u32[]{:S(2)}, u32[]{:S(2)}) collective-permute-start(f32[5,16,1,256]{3,1,0,2:T(8,128)S(1)} %copy.27), channel_id=1, source_target_pairs={{1,0},{2,1},{3,2},{4,3},{5,4},{6,5},{7,6},{8,7},{9,8},{10,9},{11,1... | collective-permute-start | bytes 245768 | tf_op jit(solution)/shard_map/ppermute | solution.py:328
  83.2 10.7 %collective-permute-start.1 = (f32[5,1,16,256]{3,2,0,1:T(8,128)S(1)}, f32[5,1,16,256]{3,2,0,1:T(8,128)S(1)}, u32[]{:S(2)}, u32[]{:S(2)}) collective-permute-start(f32[5,1,16,256]{3,2,0,1:T(8,128)S(1)} %get-tuple-element.19), channel_id=1, source_target_pairs={{16,0},{32,16},{48,32},{64,48},{80,64},{96,80},{112,96},{17,1},{33... | collective-permute-start | bytes 245768 | tf_op jit(solution)/shard_map/ppermute | solution.py:328
  85.8 8.1 %collective-permute-start = (f32[5,1,16,256]{3,2,0,1:T(8,128)S(1)}, f32[5,1,16,256]{3,2,0,1:T(8,128)S(1)}, u32[]{:S(2)}, u32[]{:S(2)}) collective-permute-start(f32[5,1,16,256]{3,2,0,1:T(8,128)S(1)} %get-tuple-element.20), channel_id=1, source_target_pairs={{0,16},{16,32},{32,48},{48,64},{64,80},{80,96},{96,112},{1,17},{17... | collective-permute-start | bytes 245768 | tf_op jit(solution)/shard_map/ppermute | solution.py:327

commit v2 on v1

--- a/solution.py
+++ b/solution.py
@@ -10,6 +10,7 @@
 F32 = jnp.float32
 BF16 = jnp.bfloat16
 I32 = jnp.int32
+MESH = pl.DeviceIdType.MESH
 
 DIFFUSION = 0.1
 CELL_MASS = 4.0
@@ -17,8 +18,12 @@
 EVAPORATION = 0.3
 LATENT_HEAT = 2.0
 
-CORNERS = tuple((u, v, w) for u in (0, 1) for v in (0, 1) for w in (0, 1))
-SHIFTS = tuple(u * 32 + v * 8 + w for u, v, w in CORNERS)
+SHIFTS = (0, 1, 8, 9, 32, 33, 40, 41)
+
+DEVICES = 128
+SLOTS = 512
+COLUMNS = 16
+HERE = 4
 
 
 def lanes():
@@ -72,8 +77,9 @@
     return blocks
 
 
-def table_kernel(gas_ref, table_ref):
+def make_table(gas_ref, table_ref):
     swaps = chunk_swaps()
+    flat_ref = table_ref.reshape(SLOTS * 4, 128)
 
     def step(n, carry):
         a, yo = n // 2, n % 2
@@ -90,20 +96,10 @@
                 for z in (0, 1):
                     for bh in (0, 1):
                         t0 = (a * 4 + yo * 2 + bh) * 32 + (h * 2 + z) * 8
-                        table_ref[pl.ds(t0 * 4 + f, 8, stride=4), :] = tiles[z][bh]
+                        flat_ref[pl.ds(t0 * 4 + f, 8, stride=4), :] = tiles[z][bh]
         return carry
 
     lax.fori_loop(0, 8, step, 0)
-
-
-def gather_kernel(index_ref, table_ref, out_ref):
-    def step(n, carry):
-        for k in range(16):
-            s = n * 16 + k
-            out_ref[s] = table_ref[index_ref[s]]
-        return carry
-
-    lax.fori_loop(0, out_ref.shape[0] // 16, step, 0)
 
 
 def split_three(ref, g):
@@ -197,20 +193,174 @@
         out_ref[pl.ds(pl.multiple_of(g * 32 + j * 8, 8), 8), :] = total
 
 
-def parcel_kernel(count_ref, tiles_ref, speed_ref, mass_ref, offset_ref, cell_ref, speed_out, mass_out, out_ref, lhs_ref, q_ref):
-    groups = mass_ref.shape[0] // 8
-
-    def first(g):
-        parcels(g, count_ref, tiles_ref, speed_ref, mass_ref, offset_ref, cell_ref, speed_out, mass_out, lhs_ref, q_ref)
-
-    def step(g, carry):
-        deposits(g - 1, lhs_ref, q_ref, out_ref)
-        first(g)
+def place():
+    gx, yz = lax.axis_index("gx"), lax.axis_index("yz")
+    return lax.div(gx, 2), lax.rem(gx, 2), lax.div(yz, 4), lax.rem(yz, 4)
+
+
+def column(turn, sign):
+    y, _, x, _ = place()
+    m = lax.rem(turn + 12, 16)
+    ox = lax.rem(m, 4)
+    oy = lax.rem(ox + lax.div(m, 4), 4)
+    return lax.rem(y + sign * oy + 4, 4), lax.rem(x + sign * ox + 4, 4)
+
+
+def members(turn, sign):
+    _, core, _, z = place()
+    y, x = column(turn, sign)
+    out = []
+    for oc in (0, 1):
+        gx = y * 2 + lax.rem(core + oc, 2)
+        for oz in range(4):
+            out.append((gx, x * 4 + lax.rem(z + oz, 4)))
+    return out
+
+
+def exchange_kernel(
+    count_ref, index_ref, gas_hbm, speed_hbm, mass_hbm, offset_hbm, cell_hbm,
+    speed_out, mass_out, arrived_ref, wanted_ref,
+    gas_ref, speed_ref, mass_ref, offset_ref, cell_ref,
+    ask_ref, got_ref, smem_ref, table_ref, send_ref, tiles_ref, deposit_ref, lhs_ref, q_ref,
+    load_sems, move_sems, tile_sems,
+):
+    me = lax.axis_index("gx") * 16 + lax.axis_index("yz")
+    barrier = pltpu.get_barrier_semaphore()
+
+    def others(turn, sign, act):
+        for n, (gx, yz) in enumerate(members(turn, sign)):
+            if n:
+                act(gx * 16 + yz, (gx, yz))
+            else:
+                pl.when(turn != HERE)(functools.partial(act, gx * 16 + yz, (gx, yz)))
+
+    def all_others(act):
+        def step(turn, carry):
+            others(turn, 1, act)
+            return carry
+
+        lax.fori_loop(0, COLUMNS, step, 0)
+
+    all_others(lambda d, to: pl.semaphore_signal(barrier, inc=1, device_id=to, device_id_type=MESH))
+    loads = [
+        pltpu.make_async_copy(src, dst, load_sems.at[n])
+        for n, (src, dst) in enumerate(
+            (
+                (gas_hbm, gas_ref),
+                (speed_hbm, speed_ref),
+                (mass_hbm, mass_ref),
+                (offset_hbm, offset_ref),
+                (cell_hbm, cell_ref),
+            )
+        )
+    ]
+    for load in loads:
+        load.start()
+    asked = jnp.concatenate([index_ref[...], jnp.zeros((124, 128), I32)], axis=0).T
+    ask_ref[:, 0, :] = asked
+    loads[0].wait()
+    make_table(gas_ref, table_ref)
+    pl.semaphore_wait(barrier, DEVICES - 1)
+
+    def move(src, dst, sem, to, arrival=None):
+        return pltpu.make_async_remote_copy(
+            src_ref=src,
+            dst_ref=dst,
+            send_sem=move_sems.at[sem],
+            recv_sem=move_sems.at[sem + 1] if arrival is None else arrival,
+            device_id=to,
+            device_id_type=MESH,
+        )
+
+    partner = (lax.axis_index("gx"), lax.rem(lax.axis_index("yz") + 1, 16))
+    all_others(lambda d, to: move(ask_ref.at[d], got_ref.at[me], 0, to).start())
+    got_ref[me] = ask_ref[me]
+    rest = pl.ds(0, DEVICES - 1)
+    asks = move(ask_ref.at[rest], got_ref.at[rest], 0, partner)
+    asks.wait_recv()
+    down = pltpu.make_async_copy(got_ref, smem_ref, load_sems.at[5])
+    down.start()
+    down.wait()
+
+    def block(ref, d):
+        return ref.at[pl.ds(pl.multiple_of(d * 16, 16), 16)]
+
+    def pick(d, dst):
+        for k in range(4):
+            dst[pl.ds(pl.multiple_of(d * 16 + k * 4, 4), 4), :] = table_ref[smem_ref[d, 0, k]]
+
+    def pick_column(turn):
+        others(turn, 1, lambda d, to: pick(d, send_ref))
+
+    def send_column(turn):
+        others(
+            turn,
+            1,
+            lambda d, to: move(block(send_ref, d), block(tiles_ref, me), 2, to, tile_sems.at[turn]).start(),
+        )
+
+    def pick_step(turn, carry):
+        pick_column(turn)
+        send_column(turn - 1)
         return carry
 
+    pick_column(0)
+    lax.fori_loop(1, COLUMNS, pick_step, 0)
+    send_column(COLUMNS - 1)
+    pick(me, tiles_ref)
+
+    for load in loads[1:]:
+        load.wait()
+
+    def await_tiles(turn):
+        def wait(slots):
+            every = pl.ds(0, slots)
+            move(send_ref.at[every], tiles_ref.at[every], 2, partner, tile_sems.at[turn]).wait_recv()
+
+        pl.when(turn == HERE)(lambda: wait(7 * 16))
+        pl.when(turn != HERE)(lambda: wait(8 * 16))
+
+    def groups(turn):
+        y, x = column(turn, -1)
+        out = []
+        for core in (0, 1):
+            g = (y * 2 + core) * 8 + x * 2
+            out += [g, g + 1]
+        return out
+
+    def first(turn):
+        for n, g in enumerate(groups(turn)):
+            parcels(g, count_ref, tiles_ref, speed_ref, mass_ref, offset_ref, cell_ref, speed_out, mass_out, lhs_ref.at[n], q_ref.at[n])
+
+    def second(turn):
+        for n, g in enumerate(groups(turn)):
+            deposits(g, lhs_ref.at[n], q_ref.at[n], deposit_ref)
+
+    def give(turn):
+        others(turn, -1, lambda d, to: move(block(deposit_ref, d), block(arrived_ref, me), 3, to).start())
+
+    def step(turn, carry):
+        await_tiles(turn)
+        second(turn - 1)
+        first(turn)
+        pl.when(turn > 1)(lambda: give(turn - 2))
+        return carry
+
+    await_tiles(0)
     first(0)
-    lax.fori_loop(1, groups, step, 0)
-    deposits(groups - 1, lhs_ref, q_ref, out_ref)
+    lax.fori_loop(1, COLUMNS, step, 0)
+    give(COLUMNS - 2)
+    second(COLUMNS - 1)
+    wanted_ref[...] = got_ref[:, 0, :].T[:8]
+    arrived_ref[pl.ds(pl.multiple_of(me * 16, 16), 16), :] = deposit_ref[pl.ds(pl.multiple_of(me * 16, 16), 16), :]
+    give(COLUMNS - 1)
+
+    asks.wait_send()
+    rest = pl.ds(0, (DEVICES - 1) * 16)
+    move(send_ref.at[rest], tiles_ref.at[rest], 2, partner).wait_send()
+    gifts = move(deposit_ref.at[rest], arrived_ref.at[rest], 3, partner)
+    gifts.wait_send()
+    gifts.wait_recv()
 
 
 def spread(plane_ref, f, x, xs, halos):
@@ -240,22 +390,24 @@
     lax.fori_loop(0, gas_ref.shape[0], step, 0)
 
 
-def scatter_kernel(index_ref, arrived_ref, *sum_refs):
-    for ref in sum_refs:
-        ref[...] = jnp.zeros_like(ref)
-
-    def step(n, carry):
+def finish_kernel(base_ref, wanted_ref, arrived_ref, out_ref, sum_ref, hit_ref):
+    lane = lanes()
+    for part in range(4):
+        at = None
         for k in range(4):
-            for m in range(4):
-                s = n * 16 + k * 4 + m
-                t = index_ref[s]
-                sum_refs[m][t] += arrived_ref[s]
-        return carry
-
-    lax.fori_loop(0, arrived_ref.shape[0] // 16, step, 0)
-
-
-def join_kernel(base_ref, s0, s1, s2, s3, out_ref):
+            row = jnp.broadcast_to(wanted_ref[pl.ds(k, 1), :], (8, 128))
+            mine = jnp.take_along_axis(row, part * 32 + lane // 4, axis=1)
+            at = mine if at is None else jnp.where(lane % 4 == k, mine, at)
+        at = jnp.broadcast_to(at[:1], (512, 128))
+        tile = lax.broadcasted_iota(I32, (512, 128), 0)
+        hit_ref[:, pl.ds(part * 128, 128)] = jnp.where(at == tile, 1.0, 0.0).astype(BF16)
+    for f in range(4):
+        value = arrived_ref[pl.ds(f, 512, stride=4), :]
+        high = value.astype(BF16)
+        rest = (value - high.astype(F32)).astype(BF16)
+        both = jnp.concatenate([high, rest], axis=1)
+        both = jnp.dot(hit_ref[...], both, preferred_element_type=F32)
+        sum_ref[f] = both[:, :128] + both[:, 128:]
     swaps = chunk_swaps()
 
     def step(n, carry):
@@ -268,8 +420,7 @@
                     tiles.append([])
                     for bh in (0, 1):
                         t0 = (a * 4 + yo * 2 + bh) * 32 + (h * 2 + z) * 8
-                        at = pl.ds(t0 * 4 + f, 8, stride=4)
-                        tiles[z].append((s0[at, :] + s1[at, :]) + (s2[at, :] + s3[at, :]))
+                        tiles[z].append(sum_ref[f, pl.ds(pl.multiple_of(t0, 8), 8), :])
                 blocks = tiles_to_grid(tiles, swaps)
                 for u in range(4):
                     at = (a * 4 + u, pl.ds(y0, 8), pl.ds(h * 128, 128))
@@ -286,9 +437,10 @@
 
 VMEM = pl.BlockSpec(memory_space=pltpu.VMEM)
 SMEM = pl.BlockSpec(memory_space=pltpu.SMEM)
-
-
-def call(kernel, name, out, in_specs, scratch=()):
+HBM = pl.BlockSpec(memory_space=pltpu.HBM)
+
+
+def call(kernel, name, out, in_specs, scratch=(), **params):
     return pl.pallas_call(
         kernel,
         name=name,
@@ -296,27 +448,17 @@
         in_specs=in_specs,
         out_specs=jax.tree.map(lambda _: VMEM, out),
         scratch_shapes=scratch,
-        compiler_params=pltpu.CompilerParams(vmem_limit_bytes=48 * 1024 * 1024),
+        compiler_params=pltpu.CompilerParams(vmem_limit_bytes=48 * 1024 * 1024, **params),
     )
 
 
-def array(*shape):
-    return jax.ShapeDtypeStruct(shape, F32)
+def array(*shape, dtype=F32):
+    return jax.ShapeDtypeStruct(shape, dtype)
 
 
 def shards(gas_state, parcel_speed, parcel_mass, offsets, cell_base, block_tile, block_count):
-    fields, xs, ys, zs = gas_state.shape
-    devices, capacity = block_tile.shape[2:]
-    slots = devices * capacity
-    tiles = xs * ys * zs // 128
-
     def three(value):
-        value = value.reshape(devices, capacity, 3, 128).transpose(0, 2, 1, 3)
-        return value.reshape(slots * 3, 128)
-
-    index = block_tile.reshape(devices, capacity)
-    wanted = lax.all_to_all(index, ("gx", "yz"), split_axis=0, concat_axis=0, tiled=True).reshape(slots)
-    table = call(table_kernel, "table", array(tiles * 4, 128), [VMEM])(gas_state)
+        return value.reshape(DEVICES, 4, 3, 128).transpose(0, 2, 1, 3).reshape(SLOTS * 3, 128)
 
     def edges(axis, dim):
         count, length = lax.axis_size(axis), gas_state.shape[dim]
@@ -329,29 +471,51 @@
         )
 
     halos = edges("gx", 1) + edges("yz", 2)
-    send = call(gather_kernel, "gather", array(slots, 4, 128), [SMEM, VMEM])(wanted, table.reshape(tiles, 4, 128))
-    fetched = lax.all_to_all(send, ("gx", "yz"), split_axis=0, concat_axis=0, tiled=True)
     base = call(diffuse_kernel, "diffuse", array(*gas_state.shape), [VMEM] * 5)(gas_state, *halos)
-    speed_next, mass_next, deposit = call(
-        parcel_kernel,
-        "parcels",
-        (array(slots * 3, 128), array(slots, 128), array(slots * 4, 128)),
-        [SMEM] + [VMEM] * 5,
-        [pltpu.VMEM((256, 128), F32), pltpu.VMEM((8, 128), I32)],
+    dma = pltpu.SemaphoreType.DMA
+    speed_next, mass_next, arrived, wanted = call(
+        exchange_kernel,
+        "exchange",
+        (array(SLOTS * 3, 128), array(SLOTS, 128), array(SLOTS * 4, 128), array(8, 128, dtype=I32)),
+        [SMEM, VMEM] + [HBM] * 5,
+        [
+            pltpu.VMEM(gas_state.shape, F32),
+            pltpu.VMEM((SLOTS * 3, 128), F32),
+            pltpu.VMEM((SLOTS, 128), F32),
+            pltpu.VMEM((SLOTS * 3, 128), F32),
+            pltpu.VMEM((SLOTS * 3, 128), I32),
+            pltpu.VMEM((DEVICES, 1, 128), I32),
+            pltpu.VMEM((DEVICES, 1, 128), I32),
+            pltpu.SMEM((DEVICES, 1, 128), I32),
+            pltpu.VMEM((SLOTS, 4, 128), F32),
+            pltpu.VMEM((SLOTS * 4, 128), F32),
+            pltpu.VMEM((SLOTS * 4, 128), F32),
+            pltpu.VMEM((SLOTS * 4, 128), F32),
+            pltpu.VMEM((4, 256, 128), F32),
+            pltpu.VMEM((4, 8, 128), I32),
+            dma((6,)),
+            dma((5,)),
+            dma((COLUMNS,)),
+        ],
+        collective_id=0,
+        has_side_effects=True,
     )(
-        block_count.reshape(devices),
-        fetched.reshape(slots * 4, 128),
+        block_count.reshape(DEVICES),
+        block_tile.reshape(DEVICES, 4).T,
+        gas_state,
         three(parcel_speed),
-        parcel_mass.reshape(slots, 128),
+        parcel_mass.reshape(SLOTS, 128),
         three(offsets),
         three(cell_base),
     )
-    arrived = lax.all_to_all(deposit.reshape(slots, 4, 128), ("gx", "yz"), split_axis=0, concat_axis=0, tiled=True)
-    sums = call(scatter_kernel, "scatter", (array(tiles, 4, 128),) * 4, [SMEM, VMEM])(wanted, arrived)
-    gas_next = call(join_kernel, "join", array(*gas_state.shape), [VMEM] * 5)(
-        base, *(one.reshape(tiles * 4, 128) for one in sums)
-    )
-    speed_next = speed_next.reshape(devices, 3, capacity, 128).transpose(0, 2, 1, 3)
+    gas_next = call(
+        finish_kernel,
+        "finish",
+        array(*gas_state.shape),
+        [VMEM] * 3,
+        [pltpu.VMEM((4, SLOTS, 128), F32), pltpu.VMEM((SLOTS, SLOTS), BF16)],
+    )(base, wanted, arrived)
+    speed_next = speed_next.reshape(DEVICES, 3, 4, 128).transpose(0, 2, 1, 3)
     return gas_next, speed_next.reshape(parcel_speed.shape), mass_next.reshape(parcel_mass.shape)
 
 

time: 103 us -> 73.9 us (0.72)
  blocking collectives: 23 us -> 0 us
  Pallas kernels: 33.3 us -> 51.2 us
  starting transfers between devices: 28 us -> 11.6 us
  waiting for transfers between devices: 12.8 us -> 0.01 us
  local copies, waits for them, and re-layouts: 3.52 us -> 9.89 us
    all_to_all x1 -> x0, blocking collectives: 23 us -> none  [shards(): lax.all_to_all(send, ('gx', 'yz'), split_axis=0, concat_axis=0, tiled=True)]
    pallas_call x5 -> x2, Pallas kernels: 32.3 us -> 50.2 us  [the longest x1 46.3 us: shards(): call(exchange_kernel, 'exchange', (array(SLOTS * 3, 128), array(SLOTS, 12...]
    all_to_all x2 -> x0, starting transfers between devices: 17.5 us -> none  [the longest x1 11.5 us: shards(): lax.all_to_all(index, ('gx', 'yz'), split_axis=0, concat_axis=0, tiled=True)]
    all_to_all x2 -> x0, waiting for transfers between devices: 7.82 us -> none  [the longest x1 6.12 us: shards(): lax.all_to_all(index, ('gx', 'yz'), split_axis=0, concat_axis=0, tiled=True)]
    unnamed x18 -> x19, local copies, waits for them, and re-layouts: 2.79 us -> 8.41 us
    ppermute x2, waiting for transfers between devices: 4.49 us -> 0.01 us  [edges(): lax.ppermute(initial, axis, [(b, a) for a, b in up])]
    slice x1, local copies, waits for them, and re-layouts: 0.12 us -> 1.48 us  [edges(): initial = lax.slice_in_dim(gas_state, 0, 1, axis=dim)]
  transfers between devices with their start and end apart: 6 -> 4, of which waited for: 4 -> 0; matrix products, arithmetic and copies ran while one was open for 0% -> 1% of each run, Pallas kernels for 3% -> 63%
where the time goes in v2:
time: 73.9 us; the launch traced here: 73.5 us
  Pallas kernels  51.2 us (69%)
  starting transfers between devices  11.6 us (16%)
  local copies, waits for them, and re-layouts  9.89 us (13%)
  between operations  0.76 us (1%)
    pallas_call x1, Pallas kernels, shards(): call(exchange_kernel, 'exchange', (array(SLOTS * 3, 128), array(SLOTS, 12...  46.3 us
    unnamed x19, local copies, waits for them, and re-layouts  8.41 us
    ppermute x2, starting transfers between devices, edges(): lax.ppermute(last, axis, up)  7.47 us
    ppermute x2, starting transfers between devices, edges(): lax.ppermute(initial, axis, [(b, a) for a, b in up])  4.16 us
    pallas_call x1, Pallas kernels, shards(): call(finish_kernel, 'finish', array(*gas_state.shape), [VMEM] * 3, [pltpu...  3.88 us
  transfers between devices with their start and end apart: 4, of which 0 were waited for; matrix products, arithmetic and copies ran while one was open for 1% of the time, Pallas kernels for 63%

profile of v2, /device:TPU:1, one launch (start us, length us, event | category | flops | bytes accessed | tf_op | source)
XLA Modules:
  0.0 73.5 jit_solution(9730312505967835434)
XLA Ops:
  0.6 0.0 copy-start.1
  0.6 1.5 %fusion = (f32[5,16,1,256]{3,2,1,0:T(1,128)S(1)}, f32[5,16,1,256]{3,2,1,0:T(1,128)S(1)}) fusion(f32[5,16,16,256]{3,2,1,0:T(8,128)} %gas_hbm.1), kind=kLoop, calls=%fused_computation.2 | loop fusion | bytes 327680 | tf_op jit(solution)/shard_map/slice | solution.py:467
  2.1 4.4 %collective-permute-start.2 = (f32[5,16,1,256]{3,1,0,2:T(8,128)S(1)}, f32[5,16,1,256]{3,1,0,2:T(8,128)S(1)}, u32[]{:S(2)}, u32[]{:S(2)}) collective-permute-start(f32[5,16,1,256]{3,1,0,2:T(8,128)S(1)} %copy.16), channel_id=1, source_target_pairs={{0,1},{1,2},{2,3},{3,4},{4,5},{5,6},{6,7},{7,8},{8,9},{9,10},{10,1... | collective-permute-start | bytes 245768 | tf_op jit(solution)/shard_map/ppermute | solution.py:469
  6.5 1.3 %collective-permute-start.3 = (f32[5,16,1,256]{3,1,0,2:T(8,128)S(1)}, f32[5,16,1,256]{3,1,0,2:T(8,128)S(1)}, u32[]{:S(2)}, u32[]{:S(2)}) collective-permute-start(f32[5,16,1,256]{3,1,0,2:T(8,128)S(1)} %copy.17), channel_id=1, source_target_pairs={{1,0},{2,1},{3,2},{4,3},{5,4},{6,5},{7,6},{8,7},{9,8},{10,9},{11,1... | collective-permute-start | bytes 245768 | tf_op jit(solution)/shard_map/ppermute | solution.py:470
  7.8 0.9 %slice_bitcast_fusion = (f32[5,1,16,256]{3,2,0,1:T(8,128)S(1)}, f32[5,1,16,256]{3,2,0,1:T(8,128)S(1)}) fusion(f32[5,16,16,256]{3,2,1,0:T(8,128)} %gas_hbm.1), kind=kLoop, calls=%fused_computation | loop fusion | bytes 327680
  8.8 2.9 %collective-permute-start.1 = (f32[5,1,16,256]{3,2,0,1:T(8,128)S(1)}, f32[5,1,16,256]{3,2,0,1:T(8,128)S(1)}, u32[]{:S(2)}, u32[]{:S(2)}) collective-permute-start(f32[5,1,16,256]{3,2,0,1:T(8,128)S(1)} %get-tuple-element.13), channel_id=1, source_target_pairs={{16,0},{32,16},{48,32},{64,48},{80,64},{96,80},{112,96},{17,1},{33... | collective-permute-start | bytes 245768 | tf_op jit(solution)/shard_map/ppermute | solution.py:470
  11.6 3.1 %collective-permute-start = (f32[5,1,16,256]{3,2,0,1:T(8,128)S(1)}, f32[5,1,16,256]{3,2,0,1:T(8,128)S(1)}, u32[]{:S(2)}, u32[]{:S(2)}) collective-permute-start(f32[5,1,16,256]{3,2,0,1:T(8,128)S(1)} %get-tuple-element.14), channel_id=1, source_target_pairs={{0,16},{16,32},{32,48},{48,64},{64,80},{80,96},{96,112},{1,17},{17... | collective-permute-start | bytes 245768 | tf_op jit(solution)/shard_map/ppermute | solution.py:469
  14.8 0.0 copy-done.1
  14.8 0.0 copy-start
  14.8 1.3 %copy-done = f32[5,16,16,256]{3,2,1,0:T(8,128)S(1)} copy-done((f32[5,16,16,256]{3,2,1,0:T(8,128)S(1)}, f32[5,16,16,256]{3,2,1,0:T(8,128)}, u32[]{:S(2)}) %copy-start) | copy-done | bytes 1310744
  16.1 1.1 %copy-done.2 = f32[1,1,128,4,3,128]{5,3,4,2,1,0:T(4,128)S(1)} copy-done((f32[1,1,128,4,3,128]{5,3,4,2,1,0:T(4,128)S(1)}, f32[1,1,128,4,3,128]{5,3,4,2,1,0:T(4,128)}, u32[]{:S(2)}) %copy-start.2) | copy-done | bytes 786456
  17.2 1.1 %copy-done.3 = s32[1,1,128,4,3,128]{5,3,4,2,1,0:T(4,128)S(1)} copy-done((s32[1,1,128,4,3,128]{5,3,4,2,1,0:T(4,128)S(1)}, s32[1,1,128,4,3,128]{5,3,4,2,1,0:T(4,128)}, u32[]{:S(2)}) %copy-start.3) | copy-done | bytes 786456
  18.4 0.9 %copy-done.4 = f32[1,1,128,4,128]{4,3,2,1,0:T(4,128)S(1)} copy-done((f32[1,1,128,4,128]{4,3,2,1,0:T(4,128)S(1)}, f32[1,1,128,4,128]{4,3,2,1,0:T(4,128)}, u32[]{:S(2)}) %copy-start.4) | copy-done | bytes 262168
  19.3 0.7 copy-done.5
  20.0 0.7 copy-done.6
  20.6 46.3 %exchange.1 = (f32[1536,128]{1,0:T(8,128)S(1)}, f32[512,128]{1,0:T(8,128)S(1)}, f32[2048,128]{1,0:T(8,128)S(1)}, s32[8,128]{1,0:T(8,128)S(1)}) custom-call(s32[128]{0:T(128)S(1)} %bitcast.45, s32[4,128]{1,0:T(4,128)S(1)} %bitcast.44, f32[5,16,16,256]{3,2,1,0:T(8,128)S(1)} %copy-done, f32[1536,128]{1,0:T(8,128)S(1)} %bitcast.35, f32[512,128]{1,0:T(8,128)S(1)} %bitcast.39, ...), custom_call_target="tpu_custom_call" | custom-call | tf_op jit(solution)/shard_map/exchange/pallas_call | solution.py:476
  66.9 0.0 collective-permute-done.2
  66.9 0.0 collective-permute-done.3
  67.0 0.0 collective-permute-done.1
  67.0 0.0 collective-permute-done
  67.0 1.1 %diffuse.1.base_ref = f32[5,16,16,256]{3,2,1,0:T(8,128)S(1)} custom-call(f32[5,16,16,256]{3,2,1,0:T(8,128)S(1)} %copy-done, f32[5,16,256]{2,1,0:T(8,128)S(1)} %bitcast.43, f32[5,16,256]{2,1,0:T(8,128)S(1)} %bitcast.42, f32[5,16,256]{2,1,0:T(8,128)S(1)} %bitcast.40, f32[5,16,256]{2,1,0:T(8,128)S(1)} %bitcast.41), custom_call_target="tpu_custom_call" | custom-call | tf_op jit(solution)/shard_map/diffuse/pallas_call | solution.py:474
  68.1 3.9 %finish.1 = f32[5,16,16,256]{3,2,1,0:T(8,128)} custom-call(f32[5,16,16,256]{3,2,1,0:T(8,128)S(1)} %diffuse.1.base_ref, s32[8,128]{1,0:T(8,128)S(1)} %get-tuple-element.7.wanted_ref, f32[2048,128]{1,0:T(8,128)S(1)} %get-tuple-element.8.arrived_ref), custom_call_target="tpu_custom_call" | custom-call | tf_op jit(solution)/shard_map/finish/pallas_call | solution.py:511
  71.9 0.9 %copy.20 = f32[1,1,128,4,3,128]{5,3,4,2,1,0:T(4,128)} copy(f32[1,1,128,4,3,128]{5,3,4,2,1,0:T(4,128)S(1)} %bitcast.34) | data formatting | bytes 1572864
  72.8 0.7 copy.21
  (7 shorter events, 0.0 us)
Async XLA Ops:
  0.6 14.1 %copy-start.1 = (f32[1,1,128,4,3,128]{5,3,4,2,1,0:T(4,128)S(1)}, f32[1,1,128,4,3,128]{5,3,4,2,1,0:T(4,128)}, u32[]{:S(2)}) copy-start(f32[1,1,128,4,3,128]{5,3,4,2,1,0:T(4,128)} %param.8) | copy-start | bytes 2359300
  2.1 64.8 %collective-permute-start.2 = (f32[5,16,1,256]{3,1,0,2:T(8,128)S(1)}, f32[5,16,1,256]{3,1,0,2:T(8,128)S(1)}, u32[]{:S(2)}, u32[]{:S(2)}) collective-permute-start(f32[5,16,1,256]{3,1,0,2:T(8,128)S(1)} %copy.16), channel_id=1, source_target_pairs={{0,1},{1,2},{2,3},{3,4},{4,5},{5,6},{6,7},{7,8},{8,9},{9,10},{10,1... | collective-permute-start | bytes 245768 | tf_op jit(solution)/shard_map/ppermute | solution.py:469
  6.5 60.4 %collective-permute-start.3 = (f32[5,16,1,256]{3,1,0,2:T(8,128)S(1)}, f32[5,16,1,256]{3,1,0,2:T(8,128)S(1)}, u32[]{:S(2)}, u32[]{:S(2)}) collective-permute-start(f32[5,16,1,256]{3,1,0,2:T(8,128)S(1)} %copy.17), channel_id=1, source_target_pairs={{1,0},{2,1},{3,2},{4,3},{5,4},{6,5},{7,6},{8,7},{9,8},{10,9},{11,1... | collective-permute-start | bytes 245768 | tf_op jit(solution)/shard_map/ppermute | solution.py:470
  8.8 58.2 %collective-permute-start.1 = (f32[5,1,16,256]{3,2,0,1:T(8,128)S(1)}, f32[5,1,16,256]{3,2,0,1:T(8,128)S(1)}, u32[]{:S(2)}, u32[]{:S(2)}) collective-permute-start(f32[5,1,16,256]{3,2,0,1:T(8,128)S(1)} %get-tuple-element.13), channel_id=1, source_target_pairs={{16,0},{32,16},{48,32},{64,48},{80,64},{96,80},{112,96},{17,1},{33... | collective-permute-start | bytes 245768 | tf_op jit(solution)/shard_map/ppermute | solution.py:470
  11.6 55.3 %collective-permute-start = (f32[5,1,16,256]{3,2,0,1:T(8,128)S(1)}, f32[5,1,16,256]{3,2,0,1:T(8,128)S(1)}, u32[]{:S(2)}, u32[]{:S(2)}) collective-permute-start(f32[5,1,16,256]{3,2,0,1:T(8,128)S(1)} %get-tuple-element.14), channel_id=1, source_target_pairs={{0,16},{16,32},{32,48},{48,64},{64,80},{80,96},{96,112},{1,17},{17... | collective-permute-start | bytes 245768 | tf_op jit(solution)/shard_map/ppermute | solution.py:469
  14.8 1.3 %copy-start = (f32[5,16,16,256]{3,2,1,0:T(8,128)S(1)}, f32[5,16,16,256]{3,2,1,0:T(8,128)}, u32[]{:S(2)}) copy-start(f32[5,16,16,256]{3,2,1,0:T(8,128)} %gas_hbm.1) | copy-start | bytes 3932164
  16.1 1.1 %copy-start.2 = (f32[1,1,128,4,3,128]{5,3,4,2,1,0:T(4,128)S(1)}, f32[1,1,128,4,3,128]{5,3,4,2,1,0:T(4,128)}, u32[]{:S(2)}) copy-start(f32[1,1,128,4,3,128]{5,3,4,2,1,0:T(4,128)} %param.10) | copy-start | bytes 2359300
  17.2 1.1 %copy-start.3 = (s32[1,1,128,4,3,128]{5,3,4,2,1,0:T(4,128)S(1)}, s32[1,1,128,4,3,128]{5,3,4,2,1,0:T(4,128)}, u32[]{:S(2)}) copy-start(s32[1,1,128,4,3,128]{5,3,4,2,1,0:T(4,128)} %param.11) | copy-start | bytes 2359300
  18.4 0.9 %copy-start.4 = (f32[1,1,128,4,128]{4,3,2,1,0:T(4,128)S(1)}, f32[1,1,128,4,128]{4,3,2,1,0:T(4,128)}, u32[]{:S(2)}) copy-start(f32[1,1,128,4,128]{4,3,2,1,0:T(4,128)} %param.9) | copy-start | bytes 786436
  19.3 0.7 copy-start.5
  20.0 0.7 copy-start.6

commit v3 on v2

--- a/solution.py
+++ b/solution.py
@@ -218,21 +218,22 @@
 
 
 def exchange_kernel(
-    count_ref, index_ref, gas_hbm, speed_hbm, mass_hbm, offset_hbm, cell_hbm,
-    speed_out, mass_out, arrived_ref, wanted_ref,
-    gas_ref, speed_ref, mass_ref, offset_ref, cell_ref,
-    ask_ref, got_ref, smem_ref, table_ref, send_ref, tiles_ref, deposit_ref, lhs_ref, q_ref,
-    load_sems, move_sems, tile_sems,
+    count_hbm, index_hbm, gas_hbm, speed_hbm, mass_hbm, offset_hbm, cell_hbm,
+    speed_out, mass_out, arrived_ref, wanted_ref, base_ref,
+    gas_ref, speed_ref, mass_ref, offset_ref, cell_ref, count_ref, index_ref,
+    ask_ref, got_ref, smem_ref, table_ref, send_ref, tiles_ref, deposit_ref, lhs_ref, q_ref, edge_ref, halo_ref,
+    load_sems, move_sems, tile_sems, edge_sems, halo_sems,
 ):
-    me = lax.axis_index("gx") * 16 + lax.axis_index("yz")
+    gx, yz = lax.axis_index("gx"), lax.axis_index("yz")
+    me = gx * 16 + yz
     barrier = pltpu.get_barrier_semaphore()
 
     def others(turn, sign, act):
-        for n, (gx, yz) in enumerate(members(turn, sign)):
+        for n, to in enumerate(members(turn, sign)):
             if n:
-                act(gx * 16 + yz, (gx, yz))
+                act(to[0] * 16 + to[1], to)
             else:
-                pl.when(turn != HERE)(functools.partial(act, gx * 16 + yz, (gx, yz)))
+                pl.when(turn != HERE)(functools.partial(act, to[0] * 16 + to[1], to))
 
     def all_others(act):
         def step(turn, carry):
@@ -241,25 +242,29 @@
 
         lax.fori_loop(0, COLUMNS, step, 0)
 
-    all_others(lambda d, to: pl.semaphore_signal(barrier, inc=1, device_id=to, device_id_type=MESH))
     loads = [
         pltpu.make_async_copy(src, dst, load_sems.at[n])
         for n, (src, dst) in enumerate(
             (
+                (index_hbm, index_ref),
                 (gas_hbm, gas_ref),
                 (speed_hbm, speed_ref),
                 (mass_hbm, mass_ref),
                 (offset_hbm, offset_ref),
                 (cell_hbm, cell_ref),
+                (count_hbm, count_ref),
             )
         )
     ]
     for load in loads:
         load.start()
+    all_others(lambda d, to: pl.semaphore_signal(barrier, inc=1, device_id=to, device_id_type=MESH))
+    loads[0].wait()
     asked = jnp.concatenate([index_ref[...], jnp.zeros((124, 128), I32)], axis=0).T
     ask_ref[:, 0, :] = asked
-    loads[0].wait()
+    loads[1].wait()
     make_table(gas_ref, table_ref)
+    make_edges(gas_ref, edge_ref)
     pl.semaphore_wait(barrier, DEVICES - 1)
 
     def move(src, dst, sem, to, arrival=None):
@@ -272,13 +277,43 @@
             device_id_type=MESH,
         )
 
-    partner = (lax.axis_index("gx"), lax.rem(lax.axis_index("yz") + 1, 16))
+    partner = (gx, lax.rem(yz + 1, 16))
     all_others(lambda d, to: move(ask_ref.at[d], got_ref.at[me], 0, to).start())
     got_ref[me] = ask_ref[me]
+
+    halos = []
+    for n, (here, there, to) in enumerate(
+        (
+            (gx < 7, gx > 0, (gx + 1, yz)),
+            (gx > 0, gx < 7, (gx - 1, yz)),
+            (yz < 15, yz > 0, (gx, yz + 1)),
+            (yz > 0, yz < 15, (gx, yz - 1)),
+        )
+    ):
+        halo = pltpu.make_async_remote_copy(
+            src_ref=edge_ref.at[n],
+            dst_ref=halo_ref.at[n],
+            send_sem=edge_sems.at[n],
+            recv_sem=halo_sems.at[n],
+            device_id=to,
+            device_id_type=MESH,
+        )
+        halos.append((here, there, halo))
+
+    def start_halos():
+        for n, (here, there, halo) in enumerate(halos):
+            pl.when(here)(halo.start)
+
+            @pl.when(jnp.logical_not(there))
+            def _(n=n):
+                halo_ref[n] = jnp.zeros(halo_ref.shape[1:], F32)
+
     rest = pl.ds(0, DEVICES - 1)
     asks = move(ask_ref.at[rest], got_ref.at[rest], 0, partner)
     asks.wait_recv()
-    down = pltpu.make_async_copy(got_ref, smem_ref, load_sems.at[5])
+    wanted_ref[...] = got_ref[:, 0, :].T[:8]
+    start_halos()
+    down = pltpu.make_async_copy(wanted_ref, smem_ref, load_sems.at[7])
     down.start()
     down.wait()
 
@@ -287,7 +322,7 @@
 
     def pick(d, dst):
         for k in range(4):
-            dst[pl.ds(pl.multiple_of(d * 16 + k * 4, 4), 4), :] = table_ref[smem_ref[d, 0, k]]
+            dst[pl.ds(pl.multiple_of(d * 16 + k * 4, 4), 4), :] = table_ref[smem_ref[k, d]]
 
     def pick_column(turn):
         others(turn, 1, lambda d, to: pick(d, send_ref))
@@ -309,8 +344,11 @@
     send_column(COLUMNS - 1)
     pick(me, tiles_ref)
 
-    for load in loads[1:]:
+    for load in loads[2:]:
         load.wait()
+    for here, there, halo in halos:
+        pl.when(there)(halo.wait_recv)
+    diffuse(gas_ref, halo_ref, base_ref)
 
     def await_tiles(turn):
         def wait(slots):
@@ -351,16 +389,30 @@
     lax.fori_loop(1, COLUMNS, step, 0)
     give(COLUMNS - 2)
     second(COLUMNS - 1)
-    wanted_ref[...] = got_ref[:, 0, :].T[:8]
-    arrived_ref[pl.ds(pl.multiple_of(me * 16, 16), 16), :] = deposit_ref[pl.ds(pl.multiple_of(me * 16, 16), 16), :]
+    mine = pl.ds(pl.multiple_of(me * 16, 16), 16)
+    arrived_ref[mine, :] = deposit_ref[mine, :]
     give(COLUMNS - 1)
 
     asks.wait_send()
+    for here, there, halo in halos:
+        pl.when(here)(halo.wait_send)
     rest = pl.ds(0, (DEVICES - 1) * 16)
     move(send_ref.at[rest], tiles_ref.at[rest], 2, partner).wait_send()
     gifts = move(deposit_ref.at[rest], arrived_ref.at[rest], 3, partner)
     gifts.wait_send()
     gifts.wait_recv()
+
+
+def make_edges(gas_ref, edge_ref):
+    def step(f, carry):
+        edge_ref[0, f] = gas_ref[f, 15]
+        edge_ref[1, f] = gas_ref[f, 0]
+        for x in range(16):
+            edge_ref[2, f, x : x + 1, :] = gas_ref[f, x, 15:16, :]
+            edge_ref[3, f, x : x + 1, :] = gas_ref[f, x, 0:1, :]
+        return carry
+
+    lax.fori_loop(0, 5, step, 0)
 
 
 def spread(plane_ref, f, x, xs, halos):
@@ -379,18 +431,24 @@
     return value + DIFFUSION * (total - 6.0 * value)
 
 
-def diffuse_kernel(gas_ref, xlo, xhi, ylo, yhi, out_ref):
+def diffuse(gas_ref, halo_ref, out_ref):
     xs = gas_ref.shape[1]
 
     def step(f, carry):
         for x in range(xs):
-            out_ref[f, x] = spread(gas_ref, f, x, xs, (xlo, xhi, ylo, yhi))
+            out_ref[f, x] = spread(gas_ref, f, x, xs, [halo_ref.at[n] for n in range(4)])
         return carry
 
     lax.fori_loop(0, gas_ref.shape[0], step, 0)
 
 
-def finish_kernel(base_ref, wanted_ref, arrived_ref, out_ref, sum_ref, hit_ref):
+def finish_kernel(base_ref, wanted_ref, arrived_ref, speed_ref, mass_ref, out_hbm, speed_hbm, mass_hbm, out_ref, sum_ref, hit_ref, sems):
+    stores = [
+        pltpu.make_async_copy(speed_ref, speed_hbm, sems.at[0]),
+        pltpu.make_async_copy(mass_ref, mass_hbm, sems.at[1]),
+    ]
+    for store in stores:
+        store.start()
     lane = lanes()
     for part in range(4):
         at = None
@@ -432,7 +490,14 @@
                         out_ref[4, *at] = base_ref[4, *at] + add
         return carry
 
-    lax.fori_loop(0, 8, step, 0)
+    for a in range(4):
+        lax.fori_loop(2 * a, 2 * a + 2, step, 0)
+        planes = pl.ds(4 * a, 4)
+        store = pltpu.make_async_copy(out_ref.at[:, planes], out_hbm.at[:, planes], sems.at[2 + a])
+        store.start()
+        stores.append(store)
+    for store in stores:
+        store.wait()
 
 
 VMEM = pl.BlockSpec(memory_space=pltpu.VMEM)
@@ -440,15 +505,15 @@
 HBM = pl.BlockSpec(memory_space=pltpu.HBM)
 
 
-def call(kernel, name, out, in_specs, scratch=(), **params):
+def call(kernel, name, out, in_specs, out_specs, scratch=(), limit=48, **params):
     return pl.pallas_call(
         kernel,
         name=name,
         out_shape=out,
         in_specs=in_specs,
-        out_specs=jax.tree.map(lambda _: VMEM, out),
+        out_specs=out_specs,
         scratch_shapes=scratch,
-        compiler_params=pltpu.CompilerParams(vmem_limit_bytes=48 * 1024 * 1024, **params),
+        compiler_params=pltpu.CompilerParams(vmem_limit_bytes=limit * 1024 * 1024, **params),
     )
 
 
@@ -460,61 +525,69 @@
     def three(value):
         return value.reshape(DEVICES, 4, 3, 128).transpose(0, 2, 1, 3).reshape(SLOTS * 3, 128)
 
-    def edges(axis, dim):
-        count, length = lax.axis_size(axis), gas_state.shape[dim]
-        up = [(i, i + 1) for i in range(count - 1)]
-        last = lax.slice_in_dim(gas_state, length - 1, length, axis=dim)
-        initial = lax.slice_in_dim(gas_state, 0, 1, axis=dim)
-        return (
-            jnp.squeeze(lax.ppermute(last, axis, up), dim),
-            jnp.squeeze(lax.ppermute(initial, axis, [(b, a) for a, b in up]), dim),
-        )
-
-    halos = edges("gx", 1) + edges("yz", 2)
-    base = call(diffuse_kernel, "diffuse", array(*gas_state.shape), [VMEM] * 5)(gas_state, *halos)
+    def hbm(value):
+        return pltpu.with_memory_space_constraint(value, pltpu.HBM)
+
     dma = pltpu.SemaphoreType.DMA
-    speed_next, mass_next, arrived, wanted = call(
+    parcel_outs = (array(SLOTS * 3, 128), array(SLOTS, 128))
+    grid = array(*gas_state.shape)
+    edge = (4, 5, 16, 256)
+    speed_next, mass_next, arrived, wanted, base = call(
         exchange_kernel,
         "exchange",
-        (array(SLOTS * 3, 128), array(SLOTS, 128), array(SLOTS * 4, 128), array(8, 128, dtype=I32)),
-        [SMEM, VMEM] + [HBM] * 5,
+        parcel_outs + (array(SLOTS * 4, 128), array(8, 128, dtype=I32), grid),
+        [HBM] * 7,
+        (VMEM,) * 5,
         [
             pltpu.VMEM(gas_state.shape, F32),
             pltpu.VMEM((SLOTS * 3, 128), F32),
             pltpu.VMEM((SLOTS, 128), F32),
             pltpu.VMEM((SLOTS * 3, 128), F32),
             pltpu.VMEM((SLOTS * 3, 128), I32),
+            pltpu.SMEM((DEVICES,), I32),
+            pltpu.VMEM((4, DEVICES), I32),
             pltpu.VMEM((DEVICES, 1, 128), I32),
             pltpu.VMEM((DEVICES, 1, 128), I32),
-            pltpu.SMEM((DEVICES, 1, 128), I32),
+            pltpu.SMEM((8, 128), I32),
             pltpu.VMEM((SLOTS, 4, 128), F32),
             pltpu.VMEM((SLOTS * 4, 128), F32),
             pltpu.VMEM((SLOTS * 4, 128), F32),
             pltpu.VMEM((SLOTS * 4, 128), F32),
             pltpu.VMEM((4, 256, 128), F32),
             pltpu.VMEM((4, 8, 128), I32),
-            dma((6,)),
+            pltpu.VMEM(edge, F32),
+            pltpu.VMEM(edge, F32),
+            dma((8,)),
             dma((5,)),
             dma((COLUMNS,)),
+            dma((4,)),
+            dma((4,)),
         ],
+        limit=48,
         collective_id=0,
         has_side_effects=True,
     )(
-        block_count.reshape(DEVICES),
-        block_tile.reshape(DEVICES, 4).T,
-        gas_state,
-        three(parcel_speed),
-        parcel_mass.reshape(SLOTS, 128),
-        three(offsets),
-        three(cell_base),
+        hbm(block_count.reshape(DEVICES)),
+        hbm(block_tile.reshape(DEVICES, 4).T),
+        hbm(gas_state),
+        hbm(three(parcel_speed)),
+        hbm(parcel_mass.reshape(SLOTS, 128)),
+        hbm(three(offsets)),
+        hbm(three(cell_base)),
     )
-    gas_next = call(
+    gas_next, speed_next, mass_next = call(
         finish_kernel,
         "finish",
-        array(*gas_state.shape),
-        [VMEM] * 3,
-        [pltpu.VMEM((4, SLOTS, 128), F32), pltpu.VMEM((SLOTS, SLOTS), BF16)],
-    )(base, wanted, arrived)
+        (grid,) + parcel_outs,
+        [VMEM] * 5,
+        (HBM,) * 3,
+        [
+            pltpu.VMEM(gas_state.shape, F32),
+            pltpu.VMEM((4, SLOTS, 128), F32),
+            pltpu.VMEM((SLOTS, SLOTS), BF16),
+            dma((6,)),
+        ],
+    )(base, wanted, arrived, speed_next, mass_next)
     speed_next = speed_next.reshape(DEVICES, 3, 4, 128).transpose(0, 2, 1, 3)
     return gas_next, speed_next.reshape(parcel_speed.shape), mass_next.reshape(parcel_mass.shape)
 

time: 73.9 us -> 52.9 us (0.72)
  starting transfers between devices: 11.6 us -> 0 us
  local copies, waits for them, and re-layouts: 9.89 us -> 0 us
    ppermute x4 -> x0, starting transfers between devices: 11.6 us -> none  [the longest x2 7.47 us: edges(): lax.ppermute(last, axis, up)]
    unnamed x19 -> x0, local copies, waits for them, and re-layouts: 8.41 us -> none
    slice x1 -> x0, local copies, waits for them, and re-layouts: 1.48 us -> none  [edges(): initial = lax.slice_in_dim(gas_state, 0, 1, axis=dim)]
    pallas_call x3 -> x2, Pallas kernels: 51.2 us -> 51.9 us  [the longest x1 48.3 us: shards(): call(exchange_kernel, 'exchange', parcel_outs + (array(SLOTS * 4, 128), a...]
  transfers between devices with their start and end apart: 4 -> 0, of which waited for: 0 -> 0; matrix products, arithmetic and copies ran while one was open for 1% -> 0% of each run, Pallas kernels for 63% -> 0%
where the time goes in v3:
time: 52.9 us; the launch traced here: 52.6 us
  Pallas kernels  51.9 us (98%)
  between operations  0.64 us (1%)
    pallas_call x1, Pallas kernels, shards(): call(exchange_kernel, 'exchange', parcel_outs + (array(SLOTS * 4, 128), a...  48.3 us
    pallas_call x1, Pallas kernels, shards(): call(finish_kernel, 'finish', (grid,) + parcel_outs, [VMEM] * 5, (HBM,) *...  3.6 us

profile of v3, /device:TPU:1, one launch (start us, length us, event | category | flops | bytes accessed | tf_op | source)
XLA Modules:
  0.0 52.6 jit_solution(714271528138100565)
XLA Ops:
  0.6 48.3 %exchange.1 = (f32[1536,128]{1,0:T(8,128)S(1)}, f32[512,128]{1,0:T(8,128)S(1)}, f32[2048,128]{1,0:T(8,128)S(1)}, s32[8,128]{1,0:T(8,128)S(1)}, f32[5,16,16,256]{3,2,1,0:T(8,128)S(1)}) custom-call(s32[128]{0:T(128)} %bitcast.31, s32[4,128]{1,0:T(4,128)} %bitcast.30, f32[5,16,16,256]{3,2,1,0:T(8,128)} %gas_hbm.1, f32[1536,128]{1,0:T(8,128)} %bitcast.26, ...), custom_call_target="tpu_custom_call" | custom-call | tf_op jit(solution)/shard_map/exchange/pallas_call | solution.py:535
  49.0 3.6 %finish.1 = (f32[5,16,16,256]{3,2,1,0:T(8,128)}, f32[1536,128]{1,0:T(8,128)}, f32[512,128]{1,0:T(8,128)}) custom-call(f32[5,16,16,256]{3,2,1,0:T(8,128)S(1)} %get-tuple-element.11.base_ref, s32[8,128]{1,0:T(8,128)S(1)} %get-tuple-element.12.wanted_ref, f32[2048,128]{1,0:T(8,128)S(1)} %get-tuple-element.13.arrived_ref, ...), custom_call_target="tpu_custom_call" | custom-call | tf_op jit(solution)/shard_map/finish/pallas_call | solution.py:578

commit v4 on v3

--- a/solution.py
+++ b/solution.py
@@ -22,8 +22,8 @@
 
 DEVICES = 128
 SLOTS = 512
-COLUMNS = 16
-HERE = 4
+TURNS = 16
+HERE = 0
 
 
 def lanes():
@@ -198,22 +198,22 @@
     return lax.div(gx, 2), lax.rem(gx, 2), lax.div(yz, 4), lax.rem(yz, 4)
 
 
-def column(turn, sign):
-    y, _, x, _ = place()
-    m = lax.rem(turn + 12, 16)
-    ox = lax.rem(m, 4)
-    oy = lax.rem(ox + lax.div(m, 4), 4)
-    return lax.rem(y + sign * oy + 4, 4), lax.rem(x + sign * ox + 4, 4)
+def pairs(turn, sign):
+    y, core, x, z = place()
+    k, oc, zb = lax.div(turn, 4), lax.rem(lax.div(turn, 2), 2), lax.rem(turn, 2)
+    out = []
+    for n in (2, 1, 3, 0):
+        gx = lax.rem(y + sign * lax.rem(k + n, 4) + 4, 4) * 2 + lax.rem(core + oc, 2)
+        out.append((gx, lax.rem(x + sign * n + 4, 4) * 4 + lax.rem(lax.div(z, 2) + zb + n, 2) * 2))
+    return out
 
 
 def members(turn, sign):
-    _, core, _, z = place()
-    y, x = column(turn, sign)
+    _, _, _, z = place()
+    mine = lax.rem(z, 2)
     out = []
-    for oc in (0, 1):
-        gx = y * 2 + lax.rem(core + oc, 2)
-        for oz in range(4):
-            out.append((gx, x * 4 + lax.rem(z + oz, 4)))
+    for gx, yz in pairs(turn, sign):
+        out += [(gx, yz + mine), (gx, yz + 1 - mine)]
     return out
 
 
@@ -222,7 +222,7 @@
     speed_out, mass_out, arrived_ref, wanted_ref, base_ref,
     gas_ref, speed_ref, mass_ref, offset_ref, cell_ref, count_ref, index_ref,
     ask_ref, got_ref, smem_ref, table_ref, send_ref, tiles_ref, deposit_ref, lhs_ref, q_ref, edge_ref, halo_ref,
-    load_sems, move_sems, tile_sems, edge_sems, halo_sems,
+    load_sems, move_sems, ask_sems, down_sems, tile_sems, edge_sems, halo_sems,
 ):
     gx, yz = lax.axis_index("gx"), lax.axis_index("yz")
     me = gx * 16 + yz
@@ -230,17 +230,17 @@
 
     def others(turn, sign, act):
         for n, to in enumerate(members(turn, sign)):
-            if n:
+            if n != 6:
                 act(to[0] * 16 + to[1], to)
             else:
                 pl.when(turn != HERE)(functools.partial(act, to[0] * 16 + to[1], to))
 
-    def all_others(act):
+    def each_turn(act):
         def step(turn, carry):
-            others(turn, 1, act)
+            act(turn)
             return carry
 
-        lax.fori_loop(0, COLUMNS, step, 0)
+        lax.fori_loop(0, TURNS, step, 0)
 
     loads = [
         pltpu.make_async_copy(src, dst, load_sems.at[n])
@@ -258,7 +258,10 @@
     ]
     for load in loads:
         load.start()
-    all_others(lambda d, to: pl.semaphore_signal(barrier, inc=1, device_id=to, device_id_type=MESH))
+    def greet(d, to):
+        pl.semaphore_signal(barrier, inc=1, device_id=to, device_id_type=MESH)
+
+    each_turn(lambda turn: others(turn, 1, greet))
     loads[0].wait()
     asked = jnp.concatenate([index_ref[...], jnp.zeros((124, 128), I32)], axis=0).T
     ask_ref[:, 0, :] = asked
@@ -278,7 +281,11 @@
         )
 
     partner = (gx, lax.rem(yz + 1, 16))
-    all_others(lambda d, to: move(ask_ref.at[d], got_ref.at[me], 0, to).start())
+
+    def ask(turn):
+        others(turn, 1, lambda d, to: move(ask_ref.at[d], got_ref.at[me], 0, to, ask_sems.at[turn]).start())
+
+    each_turn(ask)
     got_ref[me] = ask_ref[me]
 
     halos = []
@@ -308,41 +315,57 @@
             def _(n=n):
                 halo_ref[n] = jnp.zeros(halo_ref.shape[1:], F32)
 
-    rest = pl.ds(0, DEVICES - 1)
-    asks = move(ask_ref.at[rest], got_ref.at[rest], 0, partner)
-    asks.wait_recv()
-    wanted_ref[...] = got_ref[:, 0, :].T[:8]
     start_halos()
-    down = pltpu.make_async_copy(wanted_ref, smem_ref, load_sems.at[7])
-    down.start()
-    down.wait()
+
+    def await_turn(turn, sem, src, dst, per_device):
+        def wait(devices):
+            every = pl.ds(0, devices * per_device)
+            move(src.at[every], dst.at[every], sem[0], partner, sem[1].at[turn]).wait_recv()
+
+        pl.when(turn == HERE)(lambda: wait(7))
+        pl.when(turn != HERE)(lambda: wait(8))
+
+    def start_down(turn):
+        await_turn(turn, (0, ask_sems), ask_ref, got_ref, 1)
+        for x, z in pairs(turn, -1):
+            part = pl.ds(x * 16 + z, 2)
+            pltpu.make_async_copy(got_ref.at[part], smem_ref.at[part], down_sems.at[turn]).start()
+
+    def await_down(turn):
+        part = pl.ds(0, 8)
+        pltpu.make_async_copy(got_ref.at[part], smem_ref.at[part], down_sems.at[turn]).wait()
 
     def block(ref, d):
         return ref.at[pl.ds(pl.multiple_of(d * 16, 16), 16)]
 
     def pick(d, dst):
         for k in range(4):
-            dst[pl.ds(pl.multiple_of(d * 16 + k * 4, 4), 4), :] = table_ref[smem_ref[k, d]]
-
-    def pick_column(turn):
-        others(turn, 1, lambda d, to: pick(d, send_ref))
-
-    def send_column(turn):
+            dst[pl.ds(pl.multiple_of(d * 16 + k * 4, 4), 4), :] = table_ref[smem_ref[d, 0, k]]
+
+    def pick_turn(turn):
+        await_down(turn)
+        others(turn, -1, lambda d, to: pick(d, send_ref))
+
+    def send_turn(turn):
         others(
             turn,
-            1,
+            -1,
             lambda d, to: move(block(send_ref, d), block(tiles_ref, me), 2, to, tile_sems.at[turn]).start(),
         )
 
     def pick_step(turn, carry):
-        pick_column(turn)
-        send_column(turn - 1)
+        pl.when(turn < TURNS - 1)(lambda: start_down(turn + 1))
+        pick_turn(turn)
+        send_turn(turn - 1)
         return carry
 
-    pick_column(0)
-    lax.fori_loop(1, COLUMNS, pick_step, 0)
-    send_column(COLUMNS - 1)
+    start_down(0)
+    start_down(1)
+    pick_turn(0)
     pick(me, tiles_ref)
+    lax.fori_loop(1, TURNS, pick_step, 0)
+    send_turn(TURNS - 1)
+    wanted_ref[...] = got_ref[:, 0, :].T[:8]
 
     for load in loads[2:]:
         load.wait()
@@ -351,20 +374,10 @@
     diffuse(gas_ref, halo_ref, base_ref)
 
     def await_tiles(turn):
-        def wait(slots):
-            every = pl.ds(0, slots)
-            move(send_ref.at[every], tiles_ref.at[every], 2, partner, tile_sems.at[turn]).wait_recv()
-
-        pl.when(turn == HERE)(lambda: wait(7 * 16))
-        pl.when(turn != HERE)(lambda: wait(8 * 16))
+        await_turn(turn, (2, tile_sems), send_ref, tiles_ref, 16)
 
     def groups(turn):
-        y, x = column(turn, -1)
-        out = []
-        for core in (0, 1):
-            g = (y * 2 + core) * 8 + x * 2
-            out += [g, g + 1]
-        return out
+        return [x * 8 + lax.div(z, 2) for x, z in pairs(turn, 1)]
 
     def first(turn):
         for n, g in enumerate(groups(turn)):
@@ -375,7 +388,7 @@
             deposits(g, lhs_ref.at[n], q_ref.at[n], deposit_ref)
 
     def give(turn):
-        others(turn, -1, lambda d, to: move(block(deposit_ref, d), block(arrived_ref, me), 3, to).start())
+        others(turn, 1, lambda d, to: move(block(deposit_ref, d), block(arrived_ref, me), 3, to).start())
 
     def step(turn, carry):
         await_tiles(turn)
@@ -386,14 +399,15 @@
 
     await_tiles(0)
     first(0)
-    lax.fori_loop(1, COLUMNS, step, 0)
-    give(COLUMNS - 2)
-    second(COLUMNS - 1)
+    lax.fori_loop(1, TURNS, step, 0)
+    give(TURNS - 2)
+    second(TURNS - 1)
     mine = pl.ds(pl.multiple_of(me * 16, 16), 16)
     arrived_ref[mine, :] = deposit_ref[mine, :]
-    give(COLUMNS - 1)
-
-    asks.wait_send()
+    give(TURNS - 1)
+
+    rest = pl.ds(0, DEVICES - 1)
+    move(ask_ref.at[rest], got_ref.at[rest], 0, partner).wait_send()
     for here, there, halo in halos:
         pl.when(here)(halo.wait_send)
     rest = pl.ds(0, (DEVICES - 1) * 16)
@@ -468,34 +482,37 @@
         sum_ref[f] = both[:, :128] + both[:, 128:]
     swaps = chunk_swaps()
 
-    def step(n, carry):
-        a, yo = n // 2, n % 2
-        y0 = pl.multiple_of(yo * 8, 8)
-        for h in (0, 1):
-            for f in range(4):
-                tiles = []
-                for z in (0, 1):
-                    tiles.append([])
-                    for bh in (0, 1):
-                        t0 = (a * 4 + yo * 2 + bh) * 32 + (h * 2 + z) * 8
-                        tiles[z].append(sum_ref[f, pl.ds(pl.multiple_of(t0, 8), 8), :])
-                blocks = tiles_to_grid(tiles, swaps)
-                for u in range(4):
-                    at = (a * 4 + u, pl.ds(y0, 8), pl.ds(h * 128, 128))
-                    add = blocks[u] * (1.0 / CELL_MASS)
-                    if f < 3:
-                        out_ref[f, *at] = base_ref[f, *at] + add
-                    else:
-                        out_ref[3, *at] = base_ref[3, *at] - LATENT_HEAT * add
-                        out_ref[4, *at] = base_ref[4, *at] + add
+    def planes(a):
+        for yo in (0, 1):
+            for h in (0, 1):
+                for f in range(4):
+                    tiles = []
+                    for z in (0, 1):
+                        tiles.append([])
+                        for bh in (0, 1):
+                            t0 = (a * 4 + yo * 2 + bh) * 32 + (h * 2 + z) * 8
+                            tiles[z].append(sum_ref[f, pl.ds(pl.multiple_of(t0, 8), 8), :])
+                    blocks = tiles_to_grid(tiles, swaps)
+                    for u in range(4):
+                        at = (a * 4 + u, pl.ds(yo * 8, 8), pl.ds(h * 128, 128))
+                        add = blocks[u] * (1.0 / CELL_MASS)
+                        if f < 3:
+                            out_ref[f, *at] = base_ref[f, *at] + add
+                        else:
+                            out_ref[3, *at] = base_ref[3, *at] - LATENT_HEAT * add
+                            out_ref[4, *at] = base_ref[4, *at] + add
+
+    def store(a):
+        part = pl.ds(4 * a, 4)
+        return pltpu.make_async_copy(out_ref.at[:, part], out_hbm.at[:, part], sems.at[2 + a])
+
+    def step(a, carry):
+        planes(a)
+        store(a).start()
         return carry
 
-    for a in range(4):
-        lax.fori_loop(2 * a, 2 * a + 2, step, 0)
-        planes = pl.ds(4 * a, 4)
-        store = pltpu.make_async_copy(out_ref.at[:, planes], out_hbm.at[:, planes], sems.at[2 + a])
-        store.start()
-        stores.append(store)
+    lax.fori_loop(0, 4, step, 0)
+    stores += [store(a) for a in range(4)]
     for store in stores:
         store.wait()
 
@@ -548,7 +565,7 @@
             pltpu.VMEM((4, DEVICES), I32),
             pltpu.VMEM((DEVICES, 1, 128), I32),
             pltpu.VMEM((DEVICES, 1, 128), I32),
-            pltpu.SMEM((8, 128), I32),
+            pltpu.SMEM((DEVICES, 1, 128), I32),
             pltpu.VMEM((SLOTS, 4, 128), F32),
             pltpu.VMEM((SLOTS * 4, 128), F32),
             pltpu.VMEM((SLOTS * 4, 128), F32),
@@ -557,9 +574,11 @@
             pltpu.VMEM((4, 8, 128), I32),
             pltpu.VMEM(edge, F32),
             pltpu.VMEM(edge, F32),
-            dma((8,)),
+            dma((7,)),
             dma((5,)),
-            dma((COLUMNS,)),
+            dma((TURNS,)),
+            dma((TURNS,)),
+            dma((TURNS,)),
             dma((4,)),
             dma((4,)),
         ],

time: 52.9 us -> 50.2 us (0.949)
  Pallas kernels: 51.9 us -> 48.8 us
    pallas_call x1, Pallas kernels: 48.3 us -> 45.6 us  [shards(): call(exchange_kernel, 'exchange', parcel_outs + (array(SLOTS * 4, 128), a...]
where the time goes in v4:
time: 50.2 us; the launch traced here: 49.4 us
  Pallas kernels  48.8 us (97%)
  between operations  0.64 us (1%)
    pallas_call x1, Pallas kernels, shards(): call(exchange_kernel, 'exchange', parcel_outs + (array(SLOTS * 4, 128), a...  45.6 us
    pallas_call x1, Pallas kernels, shards(): call(finish_kernel, 'finish', (grid,) + parcel_outs, [VMEM] * 5, (HBM,) *...  3.13 us

profile of v4, /device:TPU:1, one launch (start us, length us, event | category | flops | bytes accessed | tf_op | source)
XLA Modules:
  0.0 49.4 jit_solution(5588714452800525697)
XLA Ops:
  0.6 45.6 %exchange.1 = (f32[1536,128]{1,0:T(8,128)S(1)}, f32[512,128]{1,0:T(8,128)S(1)}, f32[2048,128]{1,0:T(8,128)S(1)}, s32[8,128]{1,0:T(8,128)S(1)}, f32[5,16,16,256]{3,2,1,0:T(8,128)S(1)}) custom-call(s32[128]{0:T(128)} %bitcast.31, s32[4,128]{1,0:T(4,128)} %bitcast.30, f32[5,16,16,256]{3,2,1,0:T(8,128)} %gas_hbm.1, f32[1536,128]{1,0:T(8,128)} %bitcast.26, ...), custom_call_target="tpu_custom_call" | custom-call | tf_op jit(solution)/shard_map/exchange/pallas_call | solution.py:552
  46.3 3.1 %finish.1 = (f32[5,16,16,256]{3,2,1,0:T(8,128)}, f32[1536,128]{1,0:T(8,128)}, f32[512,128]{1,0:T(8,128)}) custom-call(f32[5,16,16,256]{3,2,1,0:T(8,128)S(1)} %get-tuple-element.11.base_ref, s32[8,128]{1,0:T(8,128)S(1)} %get-tuple-element.12.wanted_ref, f32[2048,128]{1,0:T(8,128)S(1)} %get-tuple-element.13.arrived_ref, ...), custom_call_target="tpu_custom_call" | custom-call | tf_op jit(solution)/shard_map/finish/pallas_call | solution.py:597

commit v5 on v4

--- a/solution.py
+++ b/solution.py
@@ -22,8 +22,49 @@
 
 DEVICES = 128
 SLOTS = 512
-TURNS = 16
-HERE = 0
+
+
+def turn_list():
+    rings = {
+        "near": ((1, 0), (3, 0), (0, 1), (0, 3)),
+        "side": ((1, 1), (3, 3), (1, 3), (3, 1)),
+        "long": ((2, 1), (2, 3), (1, 2), (3, 2)),
+    }
+    flags = ((1, 1), (0, 1), (1, 0), (0, 0))
+    here = [(0, 0, *flag) for flag in flags]
+    far = [(2, 2, *flag) for flag in flags]
+
+    def ring(name, core, z):
+        return [(y, x, core, z) for y, x in rings[name]]
+
+    def half(core):
+        return [(2, 0, core, 0), (0, 2, core, 0), (2, 0, core, 1), (0, 2, core, 1)]
+
+    return (
+        here,
+        ring("near", 0, 0),
+        ring("near", 1, 1),
+        ring("side", 0, 0),
+        half(0),
+        ring("side", 1, 1),
+        half(1),
+        ring("side", 0, 1),
+        ring("side", 1, 0),
+        ring("long", 0, 0),
+        ring("long", 1, 1),
+        ring("long", 0, 1),
+        ring("long", 1, 0),
+        far,
+        ring("near", 0, 1),
+        ring("near", 1, 0),
+    )
+
+
+ORDER = turn_list()
+TURNS = len(ORDER)
+REACH = ((0, 1), (1, 3), (3, 9), (9, 13), (13, 14))
+LATE = (14, 16)
+HERE, SELF = 0, 6
 
 
 def lanes():
@@ -77,7 +118,7 @@
     return blocks
 
 
-def make_table(gas_ref, table_ref):
+def make_table(gas_ref, table_ref, part):
     swaps = chunk_swaps()
     flat_ref = table_ref.reshape(SLOTS * 4, 128)
 
@@ -99,7 +140,7 @@
                         flat_ref[pl.ds(t0 * 4 + f, 8, stride=4), :] = tiles[z][bh]
         return carry
 
-    lax.fori_loop(0, 8, step, 0)
+    lax.fori_loop(2 * part, 2 * part + 2, step, 0)
 
 
 def split_three(ref, g):
@@ -198,13 +239,24 @@
     return lax.div(gx, 2), lax.rem(gx, 2), lax.div(yz, 4), lax.rem(yz, 4)
 
 
+def choose(turn, values):
+    if isinstance(turn, int):
+        return values[turn]
+    bit = 1
+    while len(values) > 1:
+        odd = lax.rem(lax.div(turn, bit), 2) == 1
+        values = [a if isinstance(a, int) and isinstance(b, int) and a == b else jnp.where(odd, b, a) for a, b in zip(values[::2], values[1::2])]
+        bit *= 2
+    return values[0]
+
+
 def pairs(turn, sign):
     y, core, x, z = place()
-    k, oc, zb = lax.div(turn, 4), lax.rem(lax.div(turn, 2), 2), lax.rem(turn, 2)
     out = []
-    for n in (2, 1, 3, 0):
-        gx = lax.rem(y + sign * lax.rem(k + n, 4) + 4, 4) * 2 + lax.rem(core + oc, 2)
-        out.append((gx, lax.rem(x + sign * n + 4, 4) * 4 + lax.rem(lax.div(z, 2) + zb + n, 2) * 2))
+    for n in range(4):
+        oy, ox, oc, oz = (choose(turn, [one[n][part] for one in ORDER]) for part in range(4))
+        gx = lax.rem(y + sign * oy + 4, 4) * 2 + lax.rem(core + oc, 2)
+        out.append((gx, lax.rem(x + sign * ox + 4, 4) * 4 + lax.rem(lax.div(z, 2) + oz, 2) * 2))
     return out
 
 
@@ -222,7 +274,7 @@
     speed_out, mass_out, arrived_ref, wanted_ref, base_ref,
     gas_ref, speed_ref, mass_ref, offset_ref, cell_ref, count_ref, index_ref,
     ask_ref, got_ref, smem_ref, table_ref, send_ref, tiles_ref, deposit_ref, lhs_ref, q_ref, edge_ref, halo_ref,
-    load_sems, move_sems, ask_sems, down_sems, tile_sems, edge_sems, halo_sems,
+    near_sems, load_sems, move_sems, ask_sems, down_sems, tile_sems, edge_sems, halo_sems,
 ):
     gx, yz = lax.axis_index("gx"), lax.axis_index("yz")
     me = gx * 16 + yz
@@ -230,17 +282,14 @@
 
     def others(turn, sign, act):
         for n, to in enumerate(members(turn, sign)):
-            if n != 6:
-                act(to[0] * 16 + to[1], to)
+            one = functools.partial(act, to[0] * 16 + to[1], to)
+            if n != SELF:
+                one()
+            elif isinstance(turn, int):
+                if turn != HERE:
+                    one()
             else:
-                pl.when(turn != HERE)(functools.partial(act, to[0] * 16 + to[1], to))
-
-    def each_turn(act):
-        def step(turn, carry):
-            act(turn)
-            return carry
-
-        lax.fori_loop(0, TURNS, step, 0)
+                pl.when(turn != HERE)(one)
 
     loads = [
         pltpu.make_async_copy(src, dst, load_sems.at[n])
@@ -258,18 +307,17 @@
     ]
     for load in loads:
         load.start()
-    def greet(d, to):
+    y, core, x, z = place()
+    beside = [
+        (lax.rem(y + step, 4) * 2 + core, lax.rem(x + other, 4) * 4 + z)
+        for step, other in ((1, 0), (3, 0), (0, 1), (0, 3))
+    ]
+    mates = [(y * 2 + lax.rem(core + n // 4, 2), x * 4 + lax.rem(z + n, 4)) for n in range(1, 8)]
+    for to in mates + beside:
         pl.semaphore_signal(barrier, inc=1, device_id=to, device_id_type=MESH)
-
-    each_turn(lambda turn: others(turn, 1, greet))
     loads[0].wait()
     asked = jnp.concatenate([index_ref[...], jnp.zeros((124, 128), I32)], axis=0).T
     ask_ref[:, 0, :] = asked
-    loads[1].wait()
-    make_table(gas_ref, table_ref)
-    make_edges(gas_ref, edge_ref)
-    pl.semaphore_wait(barrier, DEVICES - 1)
-
     def move(src, dst, sem, to, arrival=None):
         return pltpu.make_async_remote_copy(
             src_ref=src,
@@ -285,8 +333,25 @@
     def ask(turn):
         others(turn, 1, lambda d, to: move(ask_ref.at[d], got_ref.at[me], 0, to, ask_sems.at[turn]).start())
 
-    each_turn(ask)
+    def ask_turns(turns):
+        for turn in range(*turns):
+            ask(turn)
+
     got_ref[me] = ask_ref[me]
+    pl.semaphore_wait(barrier, len(mates + beside))
+    for n, turns in enumerate(REACH):
+        if n < 4:
+            for to in beside:
+                pl.semaphore_signal(near_sems.at[n], inc=1, device_id=to, device_id_type=MESH)
+        ask_turns(turns)
+        if n == 1:
+            ask_turns(LATE)
+        if n == 0:
+            loads[1].wait()
+        if n < 4:
+            make_table(gas_ref, table_ref, n)
+            pl.semaphore_wait(near_sems.at[n], len(beside))
+    make_edges(gas_ref, edge_ref)
 
     halos = []
     for n, (here, there, to) in enumerate(
@@ -327,8 +392,8 @@
 
     def start_down(turn):
         await_turn(turn, (0, ask_sems), ask_ref, got_ref, 1)
-        for x, z in pairs(turn, -1):
-            part = pl.ds(x * 16 + z, 2)
+        for to in pairs(turn, -1):
+            part = pl.ds(to[0] * 16 + to[1], 2)
             pltpu.make_async_copy(got_ref.at[part], smem_ref.at[part], down_sems.at[turn]).start()
 
     def await_down(turn):
@@ -377,7 +442,7 @@
         await_turn(turn, (2, tile_sems), send_ref, tiles_ref, 16)
 
     def groups(turn):
-        return [x * 8 + lax.div(z, 2) for x, z in pairs(turn, 1)]
+        return [to[0] * 8 + lax.div(to[1], 2) for to in pairs(turn, 1)]
 
     def first(turn):
         for n, g in enumerate(groups(turn)):
@@ -574,6 +639,7 @@
             pltpu.VMEM((4, 8, 128), I32),
             pltpu.VMEM(edge, F32),
             pltpu.VMEM(edge, F32),
+            pltpu.SemaphoreType.REGULAR((4,)),
             dma((7,)),
             dma((5,)),
             dma((TURNS,)),

time: 50.2 us -> 47.4 us (0.944); the launches traced: 49.4 us -> 47.3 us
  Pallas kernels: 48.8 us -> 46.7 us
    pallas_call x1, Pallas kernels: 45.6 us -> 43.5 us  [shards(): call(exchange_kernel, 'exchange', parcel_outs + (array(SLOTS * 4, 128), a...]
where the time goes in v5:
time: 47.4 us; the launch traced here: 47.3 us
  Pallas kernels  46.7 us (99%)
  between operations  0.64 us (1%)
    pallas_call x1, Pallas kernels, shards(): call(exchange_kernel, 'exchange', parcel_outs + (array(SLOTS * 4, 128), a...  43.5 us
    pallas_call x1, Pallas kernels, shards(): call(finish_kernel, 'finish', (grid,) + parcel_outs, [VMEM] * 5, (HBM,) *...  3.13 us

profile of v5, /device:TPU:1, one launch (start us, length us, event | category | flops | bytes accessed | tf_op | source)
XLA Modules:
  0.0 47.3 jit_solution(16770642531964068063)
XLA Ops:
  0.6 43.5 %exchange.1 = (f32[1536,128]{1,0:T(8,128)S(1)}, f32[512,128]{1,0:T(8,128)S(1)}, f32[2048,128]{1,0:T(8,128)S(1)}, s32[8,128]{1,0:T(8,128)S(1)}, f32[5,16,16,256]{3,2,1,0:T(8,128)S(1)}) custom-call(s32[128]{0:T(128)} %bitcast.31, s32[4,128]{1,0:T(4,128)} %bitcast.30, f32[5,16,16,256]{3,2,1,0:T(8,128)} %gas_hbm.1, f32[1536,128]{1,0:T(8,128)} %bitcast.26, ...), custom_call_target="tpu_custom_call" | custom-call | tf_op jit(solution)/shard_map/exchange/pallas_call | solution.py:617
  44.2 3.1 %finish.1 = (f32[5,16,16,256]{3,2,1,0:T(8,128)}, f32[1536,128]{1,0:T(8,128)}, f32[512,128]{1,0:T(8,128)}) custom-call(f32[5,16,16,256]{3,2,1,0:T(8,128)S(1)} %get-tuple-element.11.base_ref, s32[8,128]{1,0:T(8,128)S(1)} %get-tuple-element.12.wanted_ref, f32[2048,128]{1,0:T(8,128)S(1)} %get-tuple-element.13.arrived_ref, ...), custom_call_target="tpu_custom_call" | custom-call | tf_op jit(solution)/shard_map/finish/pallas_call | solution.py:663

commit v6 on v5

--- a/solution.py
+++ b/solution.py
@@ -315,9 +315,6 @@
     mates = [(y * 2 + lax.rem(core + n // 4, 2), x * 4 + lax.rem(z + n, 4)) for n in range(1, 8)]
     for to in mates + beside:
         pl.semaphore_signal(barrier, inc=1, device_id=to, device_id_type=MESH)
-    loads[0].wait()
-    asked = jnp.concatenate([index_ref[...], jnp.zeros((124, 128), I32)], axis=0).T
-    ask_ref[:, 0, :] = asked
     def move(src, dst, sem, to, arrival=None):
         return pltpu.make_async_remote_copy(
             src_ref=src,
@@ -337,19 +334,22 @@
         for turn in range(*turns):
             ask(turn)
 
-    got_ref[me] = ask_ref[me]
     pl.semaphore_wait(barrier, len(mates + beside))
     for n, turns in enumerate(REACH):
         if n < 4:
             for to in beside:
                 pl.semaphore_signal(near_sems.at[n], inc=1, device_id=to, device_id_type=MESH)
+        if n == 0:
+            loads[0].wait()
+            ask_ref[:, 0, :] = jnp.concatenate([index_ref[...], jnp.zeros((124, 128), I32)], axis=0).T
+            got_ref[me] = ask_ref[me]
+            loads[1].wait()
+        if n < 4:
+            make_table(gas_ref, table_ref, n)
         ask_turns(turns)
         if n == 1:
             ask_turns(LATE)
-        if n == 0:
-            loads[1].wait()
         if n < 4:
-            make_table(gas_ref, table_ref, n)
             pl.semaphore_wait(near_sems.at[n], len(beside))
     make_edges(gas_ref, edge_ref)
 
@@ -538,46 +538,46 @@
         at = jnp.broadcast_to(at[:1], (512, 128))
         tile = lax.broadcasted_iota(I32, (512, 128), 0)
         hit_ref[:, pl.ds(part * 128, 128)] = jnp.where(at == tile, 1.0, 0.0).astype(BF16)
-    for f in range(4):
+    swaps = chunk_swaps()
+
+    def add_up(f):
         value = arrived_ref[pl.ds(f, 512, stride=4), :]
         high = value.astype(BF16)
         rest = (value - high.astype(F32)).astype(BF16)
         both = jnp.concatenate([high, rest], axis=1)
         both = jnp.dot(hit_ref[...], both, preferred_element_type=F32)
         sum_ref[f] = both[:, :128] + both[:, 128:]
-    swaps = chunk_swaps()
-
-    def planes(a):
-        for yo in (0, 1):
-            for h in (0, 1):
-                for f in range(4):
-                    tiles = []
-                    for z in (0, 1):
-                        tiles.append([])
-                        for bh in (0, 1):
-                            t0 = (a * 4 + yo * 2 + bh) * 32 + (h * 2 + z) * 8
-                            tiles[z].append(sum_ref[f, pl.ds(pl.multiple_of(t0, 8), 8), :])
-                    blocks = tiles_to_grid(tiles, swaps)
-                    for u in range(4):
-                        at = (a * 4 + u, pl.ds(yo * 8, 8), pl.ds(h * 128, 128))
-                        add = blocks[u] * (1.0 / CELL_MASS)
-                        if f < 3:
-                            out_ref[f, *at] = base_ref[f, *at] + add
-                        else:
-                            out_ref[3, *at] = base_ref[3, *at] - LATENT_HEAT * add
-                            out_ref[4, *at] = base_ref[4, *at] + add
-
-    def store(a):
-        part = pl.ds(4 * a, 4)
-        return pltpu.make_async_copy(out_ref.at[:, part], out_hbm.at[:, part], sems.at[2 + a])
-
-    def step(a, carry):
-        planes(a)
-        store(a).start()
-        return carry
-
-    lax.fori_loop(0, 4, step, 0)
-    stores += [store(a) for a in range(4)]
+
+    def lay_out(f, a, yo, h):
+        tiles = []
+        for z in (0, 1):
+            tiles.append([])
+            for bh in (0, 1):
+                t0 = (a * 4 + yo * 2 + bh) * 32 + (h * 2 + z) * 8
+                tiles[z].append(sum_ref[f, pl.ds(t0, 8), :])
+        blocks = tiles_to_grid(tiles, swaps)
+        for u in range(4):
+            at = (a * 4 + u, pl.ds(yo * 8, 8), pl.ds(h * 128, 128))
+            add = blocks[u] * (1.0 / CELL_MASS)
+            if f < 3:
+                out_ref[f, *at] = base_ref[f, *at] + add
+            else:
+                out_ref[3, *at] = base_ref[3, *at] - LATENT_HEAT * add
+                out_ref[4, *at] = base_ref[4, *at] + add
+
+    order = (3, 0, 1, 2)
+    add_up(order[0])
+    for n, f in enumerate(order):
+        if n < 3:
+            add_up(order[n + 1])
+        for a in range(4):
+            for yo in (0, 1):
+                for h in (0, 1):
+                    lay_out(f, a, yo, h)
+        for field in (3, 4) if f == 3 else (f,):
+            store = pltpu.make_async_copy(out_ref.at[field], out_hbm.at[field], sems.at[2 + field])
+            store.start()
+            stores.append(store)
     for store in stores:
         store.wait()
 
@@ -670,7 +670,7 @@
             pltpu.VMEM(gas_state.shape, F32),
             pltpu.VMEM((4, SLOTS, 128), F32),
             pltpu.VMEM((SLOTS, SLOTS), BF16),
-            dma((6,)),
+            dma((7,)),
         ],
     )(base, wanted, arrived, speed_next, mass_next)
     speed_next = speed_next.reshape(DEVICES, 3, 4, 128).transpose(0, 2, 1, 3)

time: 47.4 us -> 47.2 us (level)
    pallas_call x1, Pallas kernels: 3.13 us -> 2.47 us  [shards(): call(finish_kernel, 'finish', (grid,) + parcel_outs, [VMEM] * 5, (HBM,) *...]
where the time goes in v6:
time: 47.2 us; the launch traced here: 47.1 us
  Pallas kernels  46.4 us (98%)
  between operations  0.64 us (1%)
    pallas_call x1, Pallas kernels, shards(): call(exchange_kernel, 'exchange', parcel_outs + (array(SLOTS * 4, 128), a...  44 us
    pallas_call x1, Pallas kernels, shards(): call(finish_kernel, 'finish', (grid,) + parcel_outs, [VMEM] * 5, (HBM,) *...  2.47 us

profile of v6, /device:TPU:1, one launch (start us, length us, event | category | flops | bytes accessed | tf_op | source)
XLA Modules:
  0.0 47.1 jit_solution(1534600442553733099)
XLA Ops:
  0.6 44.0 %exchange.1 = (f32[1536,128]{1,0:T(8,128)S(1)}, f32[512,128]{1,0:T(8,128)S(1)}, f32[2048,128]{1,0:T(8,128)S(1)}, s32[8,128]{1,0:T(8,128)S(1)}, f32[5,16,16,256]{3,2,1,0:T(8,128)S(1)}) custom-call(s32[128]{0:T(128)} %bitcast.31, s32[4,128]{1,0:T(4,128)} %bitcast.30, f32[5,16,16,256]{3,2,1,0:T(8,128)} %gas_hbm.1, f32[1536,128]{1,0:T(8,128)} %bitcast.26, ...), custom_call_target="tpu_custom_call" | custom-call | tf_op jit(solution)/shard_map/exchange/pallas_call | solution.py:617
  44.6 2.5 %finish.1 = (f32[5,16,16,256]{3,2,1,0:T(8,128)}, f32[1536,128]{1,0:T(8,128)}, f32[512,128]{1,0:T(8,128)}) custom-call(f32[5,16,16,256]{3,2,1,0:T(8,128)S(1)} %get-tuple-element.11.base_ref, s32[8,128]{1,0:T(8,128)S(1)} %get-tuple-element.12.wanted_ref, f32[2048,128]{1,0:T(8,128)S(1)} %get-tuple-element.13.arrived_ref, ...), custom_call_target="tpu_custom_call" | custom-call | tf_op jit(solution)/shard_map/finish/pallas_call | solution.py:663

commit v7 on v6

--- a/solution.py
+++ b/solution.py
@@ -64,7 +64,7 @@
 TURNS = len(ORDER)
 REACH = ((0, 1), (1, 3), (3, 9), (9, 13), (13, 14))
 LATE = (14, 16)
-HERE, SELF = 0, 6
+HERE, SELF = 0, 3
 
 
 def lanes():
@@ -263,10 +263,8 @@
 def members(turn, sign):
     _, _, _, z = place()
     mine = lax.rem(z, 2)
-    out = []
-    for gx, yz in pairs(turn, sign):
-        out += [(gx, yz + mine), (gx, yz + 1 - mine)]
-    return out
+    both = pairs(turn, sign)
+    return [(gx, yz + mine) for gx, yz in both] + [(gx, yz + 1 - mine) for gx, yz in both]
 
 
 def exchange_kernel(
@@ -344,11 +342,12 @@
             ask_ref[:, 0, :] = jnp.concatenate([index_ref[...], jnp.zeros((124, 128), I32)], axis=0).T
             got_ref[me] = ask_ref[me]
             loads[1].wait()
-        if n < 4:
-            make_table(gas_ref, table_ref, n)
+            make_table(gas_ref, table_ref, 0)
         ask_turns(turns)
         if n == 1:
             ask_turns(LATE)
+        if 0 < n < 4:
+            make_table(gas_ref, table_ref, n)
         if n < 4:
             pl.semaphore_wait(near_sems.at[n], len(beside))
     make_edges(gas_ref, edge_ref)

time: 47.2 us -> 46.6 us (0.987)
  Pallas kernels: 46.4 us -> 45.9 us
    pallas_call x1, Pallas kernels: 44 us -> 43.4 us  [shards(): call(exchange_kernel, 'exchange', parcel_outs + (array(SLOTS * 4, 128), a...]
where the time goes in v7:
time: 46.6 us; the launch traced here: 46.5 us
  Pallas kernels  45.9 us (98%)
  between operations  0.64 us (1%)
    pallas_call x1, Pallas kernels, shards(): call(exchange_kernel, 'exchange', parcel_outs + (array(SLOTS * 4, 128), a...  43.4 us
    pallas_call x1, Pallas kernels, shards(): call(finish_kernel, 'finish', (grid,) + parcel_outs, [VMEM] * 5, (HBM,) *...  2.47 us

profile of v7, /device:TPU:1, one launch (start us, length us, event | category | flops | bytes accessed | tf_op | source)
XLA Modules:
  0.0 46.5 jit_solution(2916433017691286254)
XLA Ops:
  0.6 43.4 %exchange.1 = (f32[1536,128]{1,0:T(8,128)S(1)}, f32[512,128]{1,0:T(8,128)S(1)}, f32[2048,128]{1,0:T(8,128)S(1)}, s32[8,128]{1,0:T(8,128)S(1)}, f32[5,16,16,256]{3,2,1,0:T(8,128)S(1)}) custom-call(s32[128]{0:T(128)} %bitcast.31, s32[4,128]{1,0:T(4,128)} %bitcast.30, f32[5,16,16,256]{3,2,1,0:T(8,128)} %gas_hbm.1, f32[1536,128]{1,0:T(8,128)} %bitcast.26, ...), custom_call_target="tpu_custom_call" | custom-call | tf_op jit(solution)/shard_map/exchange/pallas_call | solution.py:616
  44.0 2.5 %finish.1 = (f32[5,16,16,256]{3,2,1,0:T(8,128)}, f32[1536,128]{1,0:T(8,128)}, f32[512,128]{1,0:T(8,128)}) custom-call(f32[5,16,16,256]{3,2,1,0:T(8,128)S(1)} %get-tuple-element.11.base_ref, s32[8,128]{1,0:T(8,128)S(1)} %get-tuple-element.12.wanted_ref, f32[2048,128]{1,0:T(8,128)S(1)} %get-tuple-element.13.arrived_ref, ...), custom_call_target="tpu_custom_call" | custom-call | tf_op jit(solution)/shard_map/finish/pallas_call | solution.py:662
